TPU v7x, 32 devices: a whole 2x2x4 slice. The times are simulated.
32 devices in a mesh: band: 8 (over y, x, core), col: 4 (over z).
Axes of the slice: x: 2, y: 2, z: 4, core: 2. Of those that a mesh axis runs over, the one named last changes fastest.
Arguments:
- bands: float32 [4096, 8192], P(('band', 'col')), may hold values from -6 to 6
- row_interp: float32 [8, 512, 640], P('band'), may hold values from -0.25 to 0.25
- col_interp: float32 [16, 640, 512], P('col'), may hold values from -0.25 to 0.25
- row_start: int32 [8], P('band'), may hold values from 0 to 128
- col_start: int32 [16], P('col'), may hold values from 0 to 128
- spacing: float32 [8], P('band'), may hold values from 0.5 to 2
Outputs:
- elevation: float32 [4096, 8192], P('band', 'col')
- slope_sine: float32 [4096, 8192], P('band', 'col')
- hillshade: float32 [4096, 8192], P('band', 'col')
All inputs are finite; a program needn't handle non-finite values.
Results may differ from a plain program's by a relative error of at most 0.0003.
Values sent between devices are 32-bit elements; how exact they have to be, the bound alone decides.
No kernel may reach another device: no remote copies, remote signals or barrier semaphores. Data moves between devices by JAX's collectives and lax.ppermute only.
A program may use at most 128 MiB of HBM per device.

v0:
```python
import functools

import jax
import jax.numpy as jnp
from jax import lax
from jax.experimental import pallas as pl
from jax.experimental.pallas import tpu as pltpu
from jax.sharding import PartitionSpec as P


MARGIN = 128


VMEM = pltpu.VMEM
SMEM = pltpu.SMEM


def split(x):
    high = x.astype(jnp.bfloat16)
    return high, (x - high.astype(jnp.float32)).astype(jnp.bfloat16)


def dot3(a, b):
    (ah, al), (bh, bl) = a, b
    dot = functools.partial(jnp.dot, preferred_element_type=jnp.float32)
    return dot(ah, bh) + (dot(ah, bl) + dot(al, bh))


def params(mib):
    return pltpu.CompilerParams(vmem_limit_bytes=mib << 20)


def shifted_rows_kernel(start, x_ref, high_ref, low_ref):
    width = high_ref.shape[1]
    x = x_ref[0]
    x = jnp.concatenate([x, jnp.zeros((x.shape[0], width - x.shape[1]), x.dtype)], 1)
    high_ref[...], low_ref[...] = split(pltpu.roll(x, start[0], 1))


def shifted_cols_kernel(start, x_ref, high_ref, low_ref):
    count, depth, tile = high_ref.shape
    for t in range(count):
        x = x_ref[t]
        x = jnp.concatenate([x, jnp.zeros((depth - x.shape[0], tile), x.dtype)], 0)
        high_ref[t], low_ref[t] = split(pltpu.roll(x, start[t], 0))


def pad_interp(kernel, start, x, shape):
    return pl.pallas_call(
        kernel,
        out_shape=(VMEM(shape, jnp.bfloat16),) * 2,
        in_specs=[pl.BlockSpec(memory_space=SMEM), pl.BlockSpec(memory_space=VMEM)],
        out_specs=(pl.BlockSpec(memory_space=VMEM),) * 2,
        compiler_params=params(16),
    )(start, x)


def peer(i, k, n):
    return i ^ k if n & (n - 1) == 0 else (i + k) % n


def source(i, k, n):
    return i ^ k if n & (n - 1) == 0 else (i + n - k) % n


def pack_kernel(n, jobs, bands, *outs):
    me = lax.axis_index("col")
    total = bands.shape[1]
    for (k, first), out in zip(jobs, outs):
        wide = out.shape[1]
        start = jnp.clip(peer(me, k, n) * (total // n) + first, 0, total - wide)
        out[...] = bands[:, pl.ds(pl.multiple_of(start, 128), wide)]


def select_kernel(n, margin, *refs):
    slots, outs = refs[:n], refs[n:]
    me = lax.axis_index("col")
    rows = slots[0].shape[0]
    part = min(rows, margin)
    many = margin // part
    for out, owners, inner in ((outs[0], n - many, rows - part), (outs[1], 0, 0)):
        for j in range(many):
            for k in range(n):

                @pl.when(source(me, k, n) == owners + j)
                def _():
                    out[j * part : (j + 1) * part, :] = slots[k][inner : inner + part, :]


def lines_kernel(first, last, tops, bottoms, to_left, to_right):
    tile, wide = first.shape[1], tops.shape[1]
    to_left[:, :tile] = first[0:1, :]
    to_left[:, tile : tile + 128] = tops[7:8, :128]
    to_left[:, tile + 128 :] = bottoms[0:1, :128]
    to_right[:, :tile] = last[7:8, :]
    to_right[:, tile : tile + 128] = tops[7:8, wide - 128 :]
    to_right[:, tile + 128 :] = bottoms[0:1, wide - 128 :]


def tile_kernel(n, margin, t, parts, sides, doubled, held, *refs):
    slots, refs = refs[:n], refs[n:]
    others, refs = refs[: (n - 1) * doubled], refs[(n - 1) * doubled :]
    top, bottom, rh, rl, ch, cl = refs[:6]
    refs = refs[6:]
    olds = 1 + max([p[1] for p in parts if p[0] == "old"], default=-1)
    old, refs = refs[: 2 * olds], refs[2 * olds :]
    before, refs = refs[: 2 * held], refs[2 * held :]
    z, head, tail, out_h, out_l = refs[:5]
    refs = refs[5:]
    side, (high, low) = refs[:-2], refs[-2:]
    me = lax.axis_index("col")
    rows = slots[0].shape[0]
    depth = high.shape[0]
    high[0:margin, :], low[0:margin, :] = split(top[...])
    high[depth - margin : depth, :], low[depth - margin : depth, :] = split(bottom[...])
    for k, slot in enumerate(slots):
        spot = pl.ds(pl.multiple_of(margin + source(me, k, n) * rows, rows), rows)
        x = slot[...]
        if doubled and k:
            x = x + others[k - 1][...]
        high[spot, :], low[spot, :] = split(x)
    rr = dot3((rh[...], rl[...]), (high[...], low[...]))
    none = jnp.zeros((rr.shape[0], margin), rr.dtype)
    if "first" in sides:
        rr = jnp.where(me == 0, jnp.concatenate([none, rr[:, :-margin]], 1), rr)
    if "last" in sides:
        rr = jnp.where(me == n - 1, jnp.concatenate([rr[:, margin:], none], 1), rr)
    new = split(rr)
    out_h[...], out_l[...] = new
    window = ([], [])
    for part in parts:
        if part[0] == "new":
            pair = tuple(v[:, part[1] : part[2]] for v in new)
        else:
            pair = tuple(v[:, part[2] : part[3]] for v in old[2 * part[1] : 2 * part[1] + 2])
        window[0].append(pair[0])
        window[1].append(pair[1])
    window = tuple(jnp.concatenate(w, 1) for w in window)
    value = dot3(window, (ch[t], cl[t]))
    z[...] = value
    tile = value.shape[1]
    at = head.shape[1] - tile
    if held:
        head[:, :at], tail[:, :at] = before[0][...], before[1][...]
    head[:, at:] = value[:8]
    tail[:, at:] = value[value.shape[0] - 8 :]
    for ref, where in zip(side, sides):
        lanes = value[:, :128] if where == "first" else value[:, tile - 128 :]
        flipped = lanes.T
        ref[...] = flipped[:8] if where == "first" else flipped[120:]


def horn(up, now, down, scale):
    width = now.shape[1]
    s = up + 2.0 * now + down
    d = down - up
    before = lambda v: pltpu.roll(v, 1, 1)[:, 128 : width - 128]
    after = lambda v: pltpu.roll(v, width - 1, 1)[:, 128 : width - 128]
    p = (after(s) - before(s)) * scale
    q = (before(d) + 2.0 * d[:, 128 : width - 128] + after(d)) * scale
    total = p * p + q * q
    inv = lax.rsqrt(1.0 + total)
    root = total * lax.rsqrt(jnp.maximum(total, 1.2e-38))
    return root * inv, (0.70710678 - 0.5 * p + 0.5 * q) * inv


def upright(line, rows):
    return jnp.broadcast_to(line, (128, rows)).T


def cut(tiles, rows, first, last, ends):
    tile = tiles[0].shape[1]
    width = tile * len(tiles)
    pieces = [ends[0]] if first < 0 else []
    at = max(first, 0)
    while at < min(last, width):
        t, stop = at // tile, min(at // tile * tile + tile, last)
        pieces.append(tiles[t][rows, at - t * tile : stop - t * tile])
        at = stop
    if last > width:
        pieces.append(ends[1])
    return jnp.concatenate(pieces, 1)


def horn_kernel(count, ranges, fresh, held, spacing, *refs):
    tiles, (left, right) = refs[:count], refs[count : count + 2]
    elev, slope, shade, *bufs, l_col, r_col, sem_z, sem_out = refs[count + 2 + held :]
    tile = tiles[0].shape[0]
    width = tile * count
    blocks = 4 if tile % 32 == 0 else 1
    rows = tile // blocks

    def keep(j):
        return pltpu.make_async_copy(
            tiles[fresh[j]], elev.at[:, pl.ds(fresh[j] * tile, tile)], sem_z.at[j]
        )

    def store(i, b, which):
        first, last = ranges[i]
        return pltpu.make_async_copy(
            bufs[2 * i + which].at[pl.ds(b * rows, rows), :],
            (slope, shade)[which].at[pl.ds(b * rows, rows), pl.ds(first, last - first)],
            sem_out.at[i, b, which],
        )

    for j in range(len(fresh)):
        keep(j).start()
    if any(first == 0 for first, _ in ranges):
        l_col[...] = upright(left[0:1, :tile], tile)
    if any(last == width for _, last in ranges):
        r_col[...] = upright(right[0:1, :tile], tile)
    strips = tile // 8
    for i, (first, last) in enumerate(ranges):
        pieces, at = [], first
        while at < last:
            pieces.append((at, min(at + 384, last)))
            at = pieces[-1][1]
        for b in range(blocks):
            for lo, hi in pieces:
                row = lax.broadcasted_iota(jnp.int32, (8, hi - lo + 256), 0)
                scale = 0.125 / jnp.full((8, hi - lo), spacing[0])

                def load(g):
                    spot = pl.ds(pl.multiple_of(g * 8, 8), 8)
                    ends = (l_col[spot, :], r_col[spot, :])
                    return cut(tiles, spot, lo - 128, hi + 128, ends)

                def strip(r, carry):
                    g = b * (rows // 8) + r
                    before, above = carry
                    now = load(g)
                    below = load(jnp.minimum(g + 1, strips - 1))
                    rolled = pltpu.roll(now, 1, 0)
                    ahead = pltpu.roll(below, 7, 0)
                    up = jnp.where(row == 0, before, rolled)
                    down = jnp.where(row == 7, ahead, above)
                    spot = pl.ds(pl.multiple_of(g * 8, 8), 8)
                    where = pl.ds(lo - first, hi - lo)
                    bufs[2 * i][spot, where], bufs[2 * i + 1][spot, where] = horn(up, now, down, scale)
                    return rolled, ahead

                g0 = b * (rows // 8)
                start = (pltpu.roll(load(max(g0 - 1, 0)), 1, 0), pltpu.roll(load(g0), 7, 0))
                lax.fori_loop(0, rows // 8, strip, start, unroll=8)
            store(i, b, 0).start()
            store(i, b, 1).start()
    for i in range(len(ranges)):
        for b in range(blocks):
            store(i, b, 0).wait()
            store(i, b, 1).wait()
    for j in range(len(fresh)):
        keep(j).wait()


def border_kernel(count, slices, spacing, *refs):
    tiles, (left, right), refs = refs[:count], refs[count : count + 2], refs[count + 2 :]
    tops, bottoms = refs[:2], refs[2:4]
    slope, shade, buf, sem = refs[-4:]
    tile = tiles[0].shape[0]
    width = tile * count
    row = lax.broadcasted_iota(jnp.int32, (8, width + 256), 0)
    scale = 0.125 / jnp.full((8, width), spacing[0])

    def halo(groups, at):
        inner = [groups[g][at : at + 1, tile * j : tile * (j + 1)] for g, j in slices]
        side = tile if at == 7 else tile + 128
        ends = [v[0:1, side : side + 128] for v in (left, right)]
        return jnp.broadcast_to(jnp.concatenate([ends[0]] + inner + [ends[1]], 1), row.shape)

    def strip(at):
        lane = at // 128 * 128
        ends = [upright(v[0:1, lane : lane + 128], 128)[at - lane : at - lane + 8] for v in (left, right)]
        return cut(tiles, slice(at, at + 8), -128, width + 128, ends)

    copies = []
    for where, at in enumerate((0, tile - 8)):
        now = strip(at)
        above = halo(tops, 7) if where == 0 else pltpu.roll(strip(at - 8), 1, 0)
        below = halo(bottoms, 0) if where == 1 else pltpu.roll(strip(8), 7, 0)
        up = jnp.where(row == 0, above, pltpu.roll(now, 1, 0))
        down = jnp.where(row == 7, below, pltpu.roll(now, 7, 0))
        for j, (v, out) in enumerate(zip(horn(up, now, down, scale), (slope, shade))):
            buf[where, j] = v
            copies.append(
                pltpu.make_async_copy(buf.at[where, j], out.at[pl.ds(at, 8), :], sem.at[where, j])
            )
            copies[-1].start()
    for copy in copies:
        copy.wait()


def on_device(bands, row_interp, col_interp, row_start, col_start, spacing):
    n = lax.axis_size("col")
    nb = lax.axis_size("band")
    margin = MARGIN
    rows, total = bands.shape
    width = total // n
    tile = row_interp.shape[1]
    count = col_interp.shape[0]
    depth = tile + 2 * margin
    f32, bf16 = jnp.float32, jnp.bfloat16
    vm = pl.BlockSpec(memory_space=VMEM)
    sm = pl.BlockSpec(memory_space=SMEM)
    hbm = pl.BlockSpec(memory_space=pltpu.HBM)

    up = [(i, i + 1) for i in range(nb - 1)]
    down = [(i + 1, i) for i in range(nb - 1)]
    right = [(i, i + 1) for i in range(n - 1)]
    left = [(i + 1, i) for i in range(n - 1)]

    order = ([0, count - 1] if count > 1 else [0]) + list(range(1, count - 1))
    chunks, sent = [], []
    for t in order:
        free = [
            i
            for i in range(t * tile - margin, (t + 1) * tile + margin, margin)
            if not any(a <= i < b for a, b in sent)
        ]
        chunks.append((free[0], free[-1] + margin))
        sent.append(chunks[-1])

    def pack(jobs):
        return pl.pallas_call(
            functools.partial(pack_kernel, n, tuple((k, chunk[0]) for k, chunk in jobs)),
            out_shape=tuple(VMEM((rows, chunk[1] - chunk[0]), f32) for _, chunk in jobs),
            in_specs=[vm],
            out_specs=(vm,) * len(jobs),
            compiler_params=params(8),
            name="pack",
        )(bands)

    part = min(rows, margin)
    many = margin // part
    outer = [s for s in range(n) if s < many or s >= n - many]

    slots = [[None, *pack([(k, chunks[0]) for k in range(1, n)])]]
    packed = pack([(0, chunks[0])] + [(k, chunk) for chunk in chunks[1:] for k in range(n)])
    slots[0][0] = packed[0]
    slots += [list(packed[i * n + 1 : (i + 1) * n + 1]) for i in range(len(chunks) - 1)]
    rest = []
    for index, got in enumerate(slots):
        late = index > 0 and index == len(slots) - 1
        blocks = list(got)
        for k in range(n - 1, 0, -1):
            pairs = [(i, peer(i, k, n)) for i in range(n)]
            got[k] = lax.ppermute(
                blocks[k], "col", [p for p in pairs if p[0] in outer] if late else pairs
            )
            if late:
                others = [p for p in pairs if p[0] not in outer]
                rest.insert(0, lax.ppermute(blocks[k], "col", others))

    rh, rl = pad_interp(shifted_rows_kernel, row_start, row_interp, (tile, depth))
    ch, cl = pad_interp(shifted_cols_kernel, col_start, col_interp, (count, depth, tile))

    def margins_of(index):
        got = slots[index]
        last, first = pl.pallas_call(
            functools.partial(select_kernel, n, margin),
            out_shape=(VMEM((margin, got[0].shape[1]), f32),) * 2,
            in_specs=[vm] * n,
            out_specs=(vm,) * 2,
            compiler_params=params(8),
            name="select",
        )(*got)
        return lax.ppermute(last, "band", up), lax.ppermute(first, "band", down)

    groups = [[t for t in order if t in (0, count - 1)], [t for t in order if t not in (0, count - 1)]]
    group_of = lambda t: 0 if t in groups[0] else 1
    spans, rr = [], []
    ends = [None, None]
    sides = {}
    tiles = [None] * count

    def run_tile(index, t, margins):
        a0, b0 = chunks[index]
        w = b0 - a0
        spans.append((a0, b0, index))
        parts, olds = [], []
        at, high = t * tile - margin, (t + 1) * tile + margin
        while at < high:
            a, b, which = [s for s in spans if s[0] <= at < s[1]][0]
            end = min(b, high)
            if which == index:
                parts.append(("new", at - a, end - a))
            else:
                if which not in olds:
                    olds.append(which)
                parts.append(("old", olds.index(which), at - a, end - a))
            at = end
        side = [s for s, here in (("first", t == 0), ("last", t == count - 1)) if here]
        doubled = index > 0 and index == len(slots) - 1
        operands = [*slots[index]] + (rest if doubled else [])
        operands += [*margins, rh, rl, ch, cl]
        for which in olds:
            operands += rr[which]
        g = group_of(t)
        place = groups[g].index(t)
        if place:
            operands += ends[g]
        out = pl.pallas_call(
            functools.partial(
                tile_kernel, n, margin, t, tuple(parts), tuple(side), doubled, int(place > 0)
            ),
            out_shape=(
                VMEM((tile, tile), f32),
                VMEM((8, tile * (place + 1)), f32),
                VMEM((8, tile * (place + 1)), f32),
                VMEM((tile, w), bf16),
                VMEM((tile, w), bf16),
            )
            + (VMEM((8, tile), f32),) * len(side),
            in_specs=[vm] * len(operands),
            out_specs=(vm,) * (5 + len(side)),
            scratch_shapes=[VMEM((depth, w), bf16)] * 2,
            compiler_params=params(16),
        )(*operands)
        tiles[t] = out[0]
        ends[g] = (out[1], out[2])
        rr.append((out[3], out[4]))
        for s, v in zip(side, out[5:]):
            sides[s] = v

    def exchange_rows(g):
        heads, tails = ends[g]
        return lax.ppermute(tails, "band", up), lax.ppermute(heads, "band", down)

    def run_horn(ranges, fresh, held):
        some = [t for t in range(count) if tiles[t] is not None][0]
        shown = [tiles[some] if v is None else v for v in tiles]
        scratch = [VMEM((tile, last - first), f32) for first, last in ranges for _ in range(2)]
        return pl.pallas_call(
            functools.partial(horn_kernel, count, tuple(ranges), tuple(fresh), len(held)),
            out_shape=(jax.ShapeDtypeStruct((tile, width), f32),) * 3,
            in_specs=[sm] + [vm] * (count + 2) + [hbm] * len(held),
            out_specs=(hbm,) * 3,
            scratch_shapes=scratch
            + [VMEM((tile, 128), f32)] * 2
            + [
                pltpu.SemaphoreType.DMA((len(fresh),)),
                pltpu.SemaphoreType.DMA((len(ranges), 4, 2)),
            ],
            input_output_aliases={count + 3 + j: j for j in range(len(held))},
            compiler_params=params(16),
        )(spacing, *shown, *lines, *held)

    def make_lines():
        to_left, to_right = pl.pallas_call(
            lines_kernel,
            out_shape=(VMEM((1, tile + 256), f32),) * 2,
            in_specs=[vm] * 4,
            out_specs=(vm,) * 2,
            compiler_params=params(4),
            name="lines",
        )(sides["first"], sides["last"], *halos[0])
        return lax.ppermute(to_right, "col", right), lax.ppermute(to_left, "col", left)

    halos = [None, None]
    lines, maps = None, []
    for index, t in enumerate(order):
        margins = margins_of(index)
        if index > 1 and index == len(order) - 1:
            first, last = t * tile - 128, (t + 1) * tile + 128
            maps = run_horn([(0, first), (last, width)], [i for i in range(count) if i != t], [])
        run_tile(index, t, margins)
        if t == groups[0][-1]:
            halos[0] = exchange_rows(0)
            lines = make_lines()
    if groups[1]:
        halos[1] = exchange_rows(1)
        t = order[-1]
        maps = run_horn([(t * tile - 128, (t + 1) * tile + 128)], [t], list(maps))
    else:
        halos[1] = halos[0]
        maps = run_horn([(0, width)], list(range(count)), [])

    elev, *maps = maps
    where = [(group_of(t), groups[group_of(t)].index(t)) for t in range(count)]
    slope, shade = pl.pallas_call(
        functools.partial(border_kernel, count, tuple(where)),
        out_shape=(jax.ShapeDtypeStruct((tile, width), f32),) * 2,
        in_specs=[sm] + [vm] * (count + 6) + [hbm] * 2,
        out_specs=(hbm,) * 2,
        scratch_shapes=[VMEM((2, 2, 8, width), f32), pltpu.SemaphoreType.DMA((2, 2))],
        input_output_aliases={count + 7: 0, count + 8: 1},
        compiler_params=params(8),
        name="border",
    )(spacing, *tiles, *lines, halos[0][0], halos[1][0], halos[0][1], halos[1][1], *maps)
    return (elev, slope, shade)


def solution(mesh):
    in_specs = (
        P(("band", "col"), None),
        P("band", None, None),
        P("col", None, None),
        P("band"),
        P("col"),
        P("band"),
    )
    out_specs = (P("band", "col"), P("band", "col"), P("band", "col"))

    return jax.shard_map(
        on_device, mesh=mesh, in_specs=in_specs, out_specs=out_specs, check_vma=False
    )
```

profile of v0, /device:TPU:11, one launch (start us, length us, event | category | flops | bytes accessed | tf_op | source)
XLA Modules:
  0.0 197.1 jit_solution(544739960611833948)
XLA Ops:
  0.6 2.2 %copy-done = f32[128,8192]{1,0:T(8,128)S(1)} copy-done((f32[128,8192]{1,0:T(8,128)S(1)}, f32[128,8192]{1,0:T(8,128)}, u32[]{:S(2)}) %copy-start) | copy-done | bytes 4194328
  2.8 0.1 pack.3
  2.9 0.2 collective-permute-start
  3.2 0.2 pack.2
  3.4 3.3 %collective-permute-start.13 = (f32[128,256]{1,0:T(8,128)S(1)}, f32[128,256]{1,0:T(8,128)S(1)}, u32[]{:S(2)}, u32[]{:S(2)}) collective-permute-start(f32[128,256]{1,0:T(8,128)S(1)} %get-tuple-element.82), channel_id=1, source_target_pairs={{1,0},{2,3},{5,4},{6,7},{9,8},{10,11},{13,12},{14,15},{17,16},{18,... | collective-permute-start | bytes 393224 | tf_op jit(solution)/shard_map/ppermute | solution.py:351
  6.8 1.3 collective-permute-start.10
  8.1 5.1 %collective-permute-start.14 = (f32[128,256]{1,0:T(8,128)S(1)}, f32[128,256]{1,0:T(8,128)S(1)}, u32[]{:S(2)}, u32[]{:S(2)}) collective-permute-start(f32[128,256]{1,0:T(8,128)S(1)} %get-tuple-element.83), channel_id=1, source_target_pairs={{1,3},{2,0},{5,7},{6,4},{9,11},{10,8},{13,15},{14,12},{17,19},{18,... | collective-permute-start | bytes 393224 | tf_op jit(solution)/shard_map/ppermute | solution.py:351
  13.3 0.4 collective-permute-done.13.refs_4_
  13.7 7.3 %collective-permute-start.19 = (f32[128,768]{1,0:T(8,128)S(1)}, f32[128,768]{1,0:T(8,128)S(1)}, u32[]{:S(2)}, u32[]{:S(2)}) collective-permute-start(f32[128,768]{1,0:T(8,128)S(1)} %get-tuple-element.91), channel_id=1, source_target_pairs={{0,2},{1,3},{2,0},{3,1},{4,6},{5,7},{6,4},{7,5},{8,10},{9,11},{10,... | collective-permute-start | bytes 1179656 | tf_op jit(solution)/shard_map/ppermute | solution.py:346
  20.9 1.2 collective-permute-start.1
  22.1 1.2 collective-permute-start.2
  23.3 7.0 %collective-permute-done.18.refs_1_ = f32[128,768]{1,0:T(8,128)S(1)} collective-permute-done((f32[128,768]{1,0:T(8,128)S(1)}, f32[128,768]{1,0:T(8,128)S(1)}, u32[]{:S(2)}, u32[]{:S(2)}) %collective-permute-start.18) | collective-permute-done | bytes 393248 | tf_op jit(solution)/shard_map/ppermute | solution.py:346
  30.3 2.2 %collective-permute-start.5 = (f32[128,512]{1,0:T(8,128)S(1)}, f32[128,512]{1,0:T(8,128)S(1)}, u32[]{:S(2)}, u32[]{:S(2)}) collective-permute-start(f32[128,512]{1,0:T(8,128)S(1)} %get-tuple-element.73), channel_id=1, source_target_pairs={{0,1},{1,0},{2,3},{3,2},{4,5},{5,4},{6,7},{7,6},{8,9},{9,8},{10,11... | collective-permute-start | bytes 786440 | tf_op jit(solution)/shard_map/ppermute | solution.py:346
  32.5 28.8 %collective-permute-done.19.refs_2_ = f32[128,768]{1,0:T(8,128)S(1)} collective-permute-done((f32[128,768]{1,0:T(8,128)S(1)}, f32[128,768]{1,0:T(8,128)S(1)}, u32[]{:S(2)}, u32[]{:S(2)}) %collective-permute-start.19) | collective-permute-done | bytes 393248 | tf_op jit(solution)/shard_map/ppermute | solution.py:346
  61.3 3.1 %collective-permute-start.6 = (f32[128,512]{1,0:T(8,128)S(1)}, f32[128,512]{1,0:T(8,128)S(1)}, u32[]{:S(2)}, u32[]{:S(2)}) collective-permute-start(f32[128,512]{1,0:T(8,128)S(1)} %get-tuple-element.74), channel_id=1, source_target_pairs={{0,2},{1,3},{2,0},{3,1},{4,6},{5,7},{6,4},{7,5},{8,10},{9,11},{10,... | collective-permute-start | bytes 786440 | tf_op jit(solution)/shard_map/ppermute | solution.py:346
  64.4 16.6 %collective-permute-done.20.refs_3_ = f32[128,768]{1,0:T(8,128)S(1)} collective-permute-done((f32[128,768]{1,0:T(8,128)S(1)}, f32[128,768]{1,0:T(8,128)S(1)}, u32[]{:S(2)}, u32[]{:S(2)}) %collective-permute-start.20) | collective-permute-done | bytes 393248 | tf_op jit(solution)/shard_map/ppermute | solution.py:346
  81.0 2.2 %collective-permute-start.7 = (f32[128,512]{1,0:T(8,128)S(1)}, f32[128,512]{1,0:T(8,128)S(1)}, u32[]{:S(2)}, u32[]{:S(2)}) collective-permute-start(f32[128,512]{1,0:T(8,128)S(1)} %get-tuple-element.75), channel_id=1, source_target_pairs={{0,3},{1,2},{2,1},{3,0},{4,7},{5,6},{6,5},{7,4},{8,11},{9,10},{10,... | collective-permute-start | bytes 786440 | tf_op jit(solution)/shard_map/ppermute | solution.py:346
  83.3 6.1 %collective-permute-done.1.refs_2_ = f32[128,768]{1,0:T(8,128)S(1)} collective-permute-done((f32[128,768]{1,0:T(8,128)S(1)}, f32[128,768]{1,0:T(8,128)S(1)}, u32[]{:S(2)}, u32[]{:S(2)}) %collective-permute-start.1) | collective-permute-done | bytes 393248 | tf_op jit(solution)/shard_map/ppermute | solution.py:346
  89.4 8.0 %collective-permute-start.21 = (f32[128,768]{1,0:T(8,128)S(1)}, f32[128,768]{1,0:T(8,128)S(1)}, u32[]{:S(2)}, u32[]{:S(2)}) collective-permute-start(f32[128,768]{1,0:T(8,128)S(1)} %get-tuple-element.93), channel_id=1, source_target_pairs={{0,4},{4,8},{8,12},{12,16},{16,20},{20,24},{24,28},{1,5},{5,9},{9,... | collective-permute-start | bytes 1179656 | tf_op jit(solution)/shard_map/ppermute | solution.py:366
  97.5 0.4 collective-permute-done.2.refs_3_
  97.8 1.3 collective-permute-start.11
  99.1 0.1 select.4
  99.2 5.3 %collective-permute-done.11.refs_2_ = f32[128,256]{1,0:T(8,128)S(1)} collective-permute-done((f32[128,256]{1,0:T(8,128)S(1)}, f32[128,256]{1,0:T(8,128)S(1)}, u32[]{:S(2)}, u32[]{:S(2)}) %collective-permute-start.11) | collective-permute-done | bytes 131104 | tf_op jit(solution)/shard_map/ppermute | solution.py:346
  104.6 8.6 %collective-permute-start.22 = (f32[128,768]{1,0:T(8,128)S(1)}, f32[128,768]{1,0:T(8,128)S(1)}, u32[]{:S(2)}, u32[]{:S(2)}) collective-permute-start(f32[128,768]{1,0:T(8,128)S(1)} %get-tuple-element.94), channel_id=1, source_target_pairs={{4,0},{8,4},{12,8},{16,12},{20,16},{24,20},{28,24},{5,1},{9,5},{13... | collective-permute-start | bytes 1179656 | tf_op jit(solution)/shard_map/ppermute | solution.py:366
  113.2 3.0 %collective-permute-start.3 = (f32[128,768]{1,0:T(8,128)S(1)}, f32[128,768]{1,0:T(8,128)S(1)}, u32[]{:S(2)}, u32[]{:S(2)}) collective-permute-start(f32[128,768]{1,0:T(8,128)S(1)} %get-tuple-element.65), channel_id=1, source_target_pairs={{0,4},{4,8},{8,12},{12,16},{16,20},{20,24},{24,28},{1,5},{5,9},{9,... | collective-permute-start | bytes 1179656 | tf_op jit(solution)/shard_map/ppermute | solution.py:366
  116.2 1.9 collective-permute-start.4
  118.2 0.7 collective-permute-start.12
  118.9 4.5 %collective-permute-start.8 = (f32[128,512]{1,0:T(8,128)S(1)}, f32[128,512]{1,0:T(8,128)S(1)}, u32[]{:S(2)}, u32[]{:S(2)}) collective-permute-start(f32[128,512]{1,0:T(8,128)S(1)} %get-tuple-element.76), channel_id=1, source_target_pairs={{0,4},{4,8},{8,12},{12,16},{16,20},{20,24},{24,28},{1,5},{5,9},{9,... | collective-permute-start | bytes 786440 | tf_op jit(solution)/shard_map/ppermute | solution.py:366
  123.5 1.9 collective-permute-start.9
  125.5 3.6 %collective-permute-start.15 = (f32[128,256]{1,0:T(8,128)S(1)}, f32[128,256]{1,0:T(8,128)S(1)}, u32[]{:S(2)}, u32[]{:S(2)}) collective-permute-start(f32[128,256]{1,0:T(8,128)S(1)} %get-tuple-element.84), channel_id=1, source_target_pairs={{1,2},{2,1},{5,6},{6,5},{9,10},{10,9},{13,14},{14,13},{17,18},{18,... | collective-permute-start | bytes 393224 | tf_op jit(solution)/shard_map/ppermute | solution.py:351
  129.1 4.8 %collective-permute-start.16 = (f32[128,256]{1,0:T(8,128)S(1)}, f32[128,256]{1,0:T(8,128)S(1)}, u32[]{:S(2)}, u32[]{:S(2)}) collective-permute-start(f32[128,256]{1,0:T(8,128)S(1)} %get-tuple-element.85), channel_id=1, source_target_pairs={{0,4},{4,8},{8,12},{12,16},{16,20},{20,24},{24,28},{1,5},{5,9},{9,... | collective-permute-start | bytes 393224 | tf_op jit(solution)/shard_map/ppermute | solution.py:366
  133.9 2.1 %collective-permute-start.17 = (f32[128,256]{1,0:T(8,128)S(1)}, f32[128,256]{1,0:T(8,128)S(1)}, u32[]{:S(2)}, u32[]{:S(2)}) collective-permute-start(f32[128,256]{1,0:T(8,128)S(1)} %get-tuple-element.86), channel_id=1, source_target_pairs={{4,0},{8,4},{12,8},{16,12},{20,16},{24,20},{28,24},{5,1},{9,5},{13... | collective-permute-start | bytes 393224 | tf_op jit(solution)/shard_map/ppermute | solution.py:366
  136.7 1.1 shard_map.85
  137.9 4.7 %shard_map.86 = (bf16[4,768,512]{2,1,0:T(8,128)(2,1)S(1)}, bf16[4,768,512]{2,1,0:T(8,128)(2,1)S(1)}) custom-call(s32[4]{0:T(128)S(1)} %copy-done.2, f32[4,640,512]{2,1,0:T(8,128)S(1)} %bitcast.1), custom_call_target="tpu_custom_call" | custom-call | tf_op jit(solution)/shard_map/pallas_call | solution.py:49
  142.6 5.8 %shard_map.87 = (f32[512,512]{1,0:T(8,128)S(1)}, f32[8,512]{1,0:T(8,128)S(1)}, f32[8,512]{1,0:T(8,128)S(1)}, bf16[512,768]{1,0:T(8,128)(2,1)S(1)}, bf16[512,768]{1,0:T(8,128)(2,1)S(1)}, /*index=5*/f32[8,512]{1,0:T(8,128)S(1)}) custom-call(f32[128,768]{1,0:T(8,128)S(1)} %get-tuple-element.61.refs_0_, f32[128,768]{1,0:T(8,128)S(1)} %collective-permute-done.refs_1_, ...), custom_call_target="tpu_custom_call" | custom-call | tf_op jit(solution)/shard_map/pallas_call | solution.py:401
  148.5 6.2 %shard_map.89 = (f32[512,512]{1,0:T(8,128)S(1)}, f32[8,1024]{1,0:T(8,128)S(1)}, f32[8,1024]{1,0:T(8,128)S(1)}, bf16[512,768]{1,0:T(8,128)(2,1)S(1)}, bf16[512,768]{1,0:T(8,128)(2,1)S(1)}, /*index=5*/f32[8,512]{1,0:T(8,128)S(1)}) custom-call(f32[128,768]{1,0:T(8,128)S(1)} %get-tuple-element.89.refs_0_, f32[128,768]{1,0:T(8,128)S(1)} %collective-permute-done.18.refs_1_, ...), custom_call_target="tpu_custom_call" | custom-call | tf_op jit(solution)/shard_map/pallas_call | solution.py:401
  154.7 4.5 %collective-permute-start.23 = (f32[8,1024]{1,0:T(8,128)S(1)}, f32[8,1024]{1,0:T(8,128)S(1)}, u32[]{:S(2)}, u32[]{:S(2)}) collective-permute-start(f32[8,1024]{1,0:T(8,128)S(1)} %get-tuple-element.105), channel_id=1, source_target_pairs={{0,4},{4,8},{8,12},{12,16},{16,20},{20,24},{24,28},{1,5},{5,9},{9,... | collective-permute-start | bytes 98312 | tf_op jit(solution)/shard_map/ppermute | solution.py:426
  159.3 1.9 collective-permute-start.24
  161.2 2.9 %shard_map.88 = (f32[512,512]{1,0:T(8,128)S(1)}, f32[8,512]{1,0:T(8,128)S(1)}, f32[8,512]{1,0:T(8,128)S(1)}, bf16[512,512]{1,0:T(8,128)(2,1)S(1)}, bf16[512,512]{1,0:T(8,128)(2,1)S(1)}) custom-call(f32[128,512]{1,0:T(8,128)S(1)} %get-tuple-element.72.refs_0_, f32[128,512]{1,0:T(8,128)S(1)} %collective-permute-done.5.refs_1_, ...), custom_call_target="tpu_custom_call" | custom-call | tf_op jit(solution)/shard_map/pallas_call | solution.py:401
  164.1 4.0 %shard_map.90 = (f32[512,512]{1,0:T(8,128)S(1)}, f32[8,1024]{1,0:T(8,128)S(1)}, f32[8,1024]{1,0:T(8,128)S(1)}, bf16[512,256]{1,0:T(8,128)(2,1)}, bf16[512,256]{1,0:T(8,128)(2,1)}) custom-call(f32[128,256]{1,0:T(8,128)S(1)} %get-tuple-element.81.refs_0_, f32[128,256]{1,0:T(8,128)S(1)} %collective-permute-done.10.refs_1_, ...), custom_call_target="tpu_custom_call" | custom-call | tf_op jit(solution)/shard_map/pallas_call | solution.py:401
  168.1 4.5 %collective-permute-start.27 = (f32[8,1024]{1,0:T(8,128)S(1)}, f32[8,1024]{1,0:T(8,128)S(1)}, u32[]{:S(2)}, u32[]{:S(2)}) collective-permute-start(f32[8,1024]{1,0:T(8,128)S(1)} %get-tuple-element.113), channel_id=1, source_target_pairs={{0,4},{4,8},{8,12},{12,16},{16,20},{20,24},{24,28},{1,5},{5,9},{9,... | collective-permute-start | bytes 98312 | tf_op jit(solution)/shard_map/ppermute | solution.py:426
  172.7 1.9 collective-permute-start.28
  174.6 1.9 collective-permute-start.25
  176.6 5.7 %collective-permute-start.26 = (f32[1,768]{1,0:T(1,128)S(1)}, f32[1,768]{1,0:T(1,128)S(1)}, u32[]{:S(2)}, u32[]{:S(2)}) collective-permute-start(f32[1,768]{1,0:T(1,128)S(1)} %get-tuple-element.108), channel_id=1, source_target_pairs={{1,0},{2,1},{3,2},{5,4},{6,5},{7,6},{9,8},{10,9},{11,10},{13,12},{... | collective-permute-start | bytes 9224 | tf_op jit(solution)/shard_map/ppermute | solution.py:456
  182.9 0.7 collective-permute-done.26.refs_5_
  183.6 7.7 %shard_map.91 = (f32[512,2048]{1,0:T(8,128)}, f32[512,2048]{1,0:T(8,128)}, f32[512,2048]{1,0:T(8,128)}) custom-call(f32[1]{0:T(128)S(6)} %copy.20.spacing, f32[512,512]{1,0:T(8,128)S(1)} %get-tuple-element.71.refs_0_.refs_2_, f32[512,512]{1,0:T(8,128)S(1)} %get-tuple-element.80.refs_1_, f32[512,512]{1,0:T(8,128)S(1)} %get-tuple-element.71.refs_0_.refs_2_, ...), custom_call_target="tpu_custom_call" | custom-call | tf_op jit(solution)/shard_map/pallas_call | solution.py:432
  191.3 4.6 %shard_map.92 = (f32[512,2048]{1,0:T(8,128)}, f32[512,2048]{1,0:T(8,128)}, f32[512,2048]{1,0:T(8,128)}) custom-call(f32[1]{0:T(128)S(6)} %copy.20.spacing, f32[512,512]{1,0:T(8,128)S(1)} %get-tuple-element.71.refs_0_.refs_2_, f32[512,512]{1,0:T(8,128)S(1)} %get-tuple-element.80.refs_1_, ...), custom_call_target="tpu_custom_call", output_to_operand_aliasing={{0}: (7, {}), {1}: (8, {}), {2}: (9, {})} | custom-call | tf_op jit(solution)/shard_map/pallas_call | solution.py:432
  195.9 1.0 border.1
  (37 shorter events, 0.4 us)
Async XLA Ops:
  0.6 2.2 %copy-start = (f32[128,8192]{1,0:T(8,128)S(1)}, f32[128,8192]{1,0:T(8,128)}, u32[]{:S(2)}) copy-start(f32[128,8192]{1,0:T(8,128)} %bands.3) | copy-start | bytes 12582916
  2.8 135.0 %slice-start = ((s8[5242880]{0:T(1024)(128)(4,1)}), s8[4194304]{0:T(1024)(128)(4,1)S(1)}, s32[]{:S(2)}) async-start(s8[5242880]{0:T(1024)(128)(4,1)} %bitcast), calls=%async_computation | async-start | bytes 8388608
  2.9 133.8 %copy-start.1 = (f32[1,512,640]{2,1,0:T(8,128)S(1)}, f32[1,512,640]{2,1,0:T(8,128)}, u32[]{:S(2)}) copy-start(f32[1,512,640]{2,1,0:T(8,128)} %x_ref.2) | copy-start | bytes 3932164
  2.9 135.0 %slice-start.1 = ((s8[5242880]{0:T(1024)(128)(4,1)}), s8[1048576]{0:T(1024)(128)(4,1)S(1)}, s32[]{:S(2)}) async-start(s8[5242880]{0:T(1024)(128)(4,1)} %bitcast), calls=%async_computation.1 | async-start | bytes 2097152
  2.9 134.9 %copy-start.2 = (s32[4]{0:T(128)S(1)}, s32[4]{0:T(128)}, u32[]{:S(2)}) copy-start(s32[4]{0:T(128)} %start.2) | copy-start | bytes 52
  2.9 19.2 %collective-permute-start = (f32[128,768]{1,0:T(8,128)S(1)}, f32[128,768]{1,0:T(8,128)S(1)}, u32[]{:S(2)}, u32[]{:S(2)}) collective-permute-start(f32[128,768]{1,0:T(8,128)S(1)} %get-tuple-element.62), channel_id=1, source_target_pairs={{0,1},{1,0},{2,3},{3,2},{4,5},{5,4},{6,7},{7,6},{8,9},{9,8},{10,11... | collective-permute-start | bytes 1179656 | tf_op jit(solution)/shard_map/ppermute | solution.py:346
  3.4 10.2 %collective-permute-start.13 = (f32[128,256]{1,0:T(8,128)S(1)}, f32[128,256]{1,0:T(8,128)S(1)}, u32[]{:S(2)}, u32[]{:S(2)}) collective-permute-start(f32[128,256]{1,0:T(8,128)S(1)} %get-tuple-element.82), channel_id=1, source_target_pairs={{1,0},{2,3},{5,4},{6,7},{9,8},{10,11},{13,12},{14,15},{17,16},{18,... | collective-permute-start | bytes 393224 | tf_op jit(solution)/shard_map/ppermute | solution.py:351
  6.8 14.2 %collective-permute-start.10 = (f32[128,256]{1,0:T(8,128)S(1)}, f32[128,256]{1,0:T(8,128)S(1)}, u32[]{:S(2)}, u32[]{:S(2)}) collective-permute-start(f32[128,256]{1,0:T(8,128)S(1)} %get-tuple-element.82), channel_id=1, source_target_pairs={{0,1},{3,2},{4,5},{7,6},{8,9},{11,10},{12,13},{15,14},{16,17},{19,... | collective-permute-start | bytes 393224 | tf_op jit(solution)/shard_map/ppermute | solution.py:346
  8.1 12.9 %collective-permute-start.14 = (f32[128,256]{1,0:T(8,128)S(1)}, f32[128,256]{1,0:T(8,128)S(1)}, u32[]{:S(2)}, u32[]{:S(2)}) collective-permute-start(f32[128,256]{1,0:T(8,128)S(1)} %get-tuple-element.83), channel_id=1, source_target_pairs={{1,3},{2,0},{5,7},{6,4},{9,11},{10,8},{13,15},{14,12},{17,19},{18,... | collective-permute-start | bytes 393224 | tf_op jit(solution)/shard_map/ppermute | solution.py:351
  13.2 17.1 %collective-permute-start.18 = (f32[128,768]{1,0:T(8,128)S(1)}, f32[128,768]{1,0:T(8,128)S(1)}, u32[]{:S(2)}, u32[]{:S(2)}) collective-permute-start(f32[128,768]{1,0:T(8,128)S(1)} %get-tuple-element.90), channel_id=1, source_target_pairs={{0,1},{1,0},{2,3},{3,2},{4,5},{5,4},{6,7},{7,6},{8,9},{9,8},{10,11... | collective-permute-start | bytes 1179656 | tf_op jit(solution)/shard_map/ppermute | solution.py:346
  13.7 47.7 %collective-permute-start.19 = (f32[128,768]{1,0:T(8,128)S(1)}, f32[128,768]{1,0:T(8,128)S(1)}, u32[]{:S(2)}, u32[]{:S(2)}) collective-permute-start(f32[128,768]{1,0:T(8,128)S(1)} %get-tuple-element.91), channel_id=1, source_target_pairs={{0,2},{1,3},{2,0},{3,1},{4,6},{5,7},{6,4},{7,5},{8,10},{9,11},{10,... | collective-permute-start | bytes 1179656 | tf_op jit(solution)/shard_map/ppermute | solution.py:346
  20.9 60.1 %collective-permute-start.20 = (f32[128,768]{1,0:T(8,128)S(1)}, f32[128,768]{1,0:T(8,128)S(1)}, u32[]{:S(2)}, u32[]{:S(2)}) collective-permute-start(f32[128,768]{1,0:T(8,128)S(1)} %get-tuple-element.92), channel_id=1, source_target_pairs={{0,3},{1,2},{2,1},{3,0},{4,7},{5,6},{6,5},{7,4},{8,11},{9,10},{10,... | collective-permute-start | bytes 1179656 | tf_op jit(solution)/shard_map/ppermute | solution.py:346
  20.9 68.5 %collective-permute-start.1 = (f32[128,768]{1,0:T(8,128)S(1)}, f32[128,768]{1,0:T(8,128)S(1)}, u32[]{:S(2)}, u32[]{:S(2)}) collective-permute-start(f32[128,768]{1,0:T(8,128)S(1)} %get-tuple-element.63), channel_id=1, source_target_pairs={{0,2},{1,3},{2,0},{3,1},{4,6},{5,7},{6,4},{7,5},{8,10},{9,11},{10,... | collective-permute-start | bytes 1179656 | tf_op jit(solution)/shard_map/ppermute | solution.py:346
  22.1 75.7 %collective-permute-start.2 = (f32[128,768]{1,0:T(8,128)S(1)}, f32[128,768]{1,0:T(8,128)S(1)}, u32[]{:S(2)}, u32[]{:S(2)}) collective-permute-start(f32[128,768]{1,0:T(8,128)S(1)} %get-tuple-element.64), channel_id=1, source_target_pairs={{0,3},{1,2},{2,1},{3,0},{4,7},{5,6},{6,5},{7,4},{8,11},{9,10},{10,... | collective-permute-start | bytes 1179656 | tf_op jit(solution)/shard_map/ppermute | solution.py:346
  30.3 82.9 %collective-permute-start.5 = (f32[128,512]{1,0:T(8,128)S(1)}, f32[128,512]{1,0:T(8,128)S(1)}, u32[]{:S(2)}, u32[]{:S(2)}) collective-permute-start(f32[128,512]{1,0:T(8,128)S(1)} %get-tuple-element.73), channel_id=1, source_target_pairs={{0,1},{1,0},{2,3},{3,2},{4,5},{5,4},{6,7},{7,6},{8,9},{9,8},{10,11... | collective-permute-start | bytes 786440 | tf_op jit(solution)/shard_map/ppermute | solution.py:346
  61.3 54.9 %collective-permute-start.6 = (f32[128,512]{1,0:T(8,128)S(1)}, f32[128,512]{1,0:T(8,128)S(1)}, u32[]{:S(2)}, u32[]{:S(2)}) collective-permute-start(f32[128,512]{1,0:T(8,128)S(1)} %get-tuple-element.74), channel_id=1, source_target_pairs={{0,2},{1,3},{2,0},{3,1},{4,6},{5,7},{6,4},{7,5},{8,10},{9,11},{10,... | collective-permute-start | bytes 786440 | tf_op jit(solution)/shard_map/ppermute | solution.py:346
  81.0 37.2 %collective-permute-start.7 = (f32[128,512]{1,0:T(8,128)S(1)}, f32[128,512]{1,0:T(8,128)S(1)}, u32[]{:S(2)}, u32[]{:S(2)}) collective-permute-start(f32[128,512]{1,0:T(8,128)S(1)} %get-tuple-element.75), channel_id=1, source_target_pairs={{0,3},{1,2},{2,1},{3,0},{4,7},{5,6},{6,5},{7,4},{8,11},{9,10},{10,... | collective-permute-start | bytes 786440 | tf_op jit(solution)/shard_map/ppermute | solution.py:346
  89.4 34.1 %collective-permute-start.21 = (f32[128,768]{1,0:T(8,128)S(1)}, f32[128,768]{1,0:T(8,128)S(1)}, u32[]{:S(2)}, u32[]{:S(2)}) collective-permute-start(f32[128,768]{1,0:T(8,128)S(1)} %get-tuple-element.93), channel_id=1, source_target_pairs={{0,4},{4,8},{8,12},{12,16},{16,20},{20,24},{24,28},{1,5},{5,9},{9,... | collective-permute-start | bytes 1179656 | tf_op jit(solution)/shard_map/ppermute | solution.py:366
  97.8 6.7 %collective-permute-start.11 = (f32[128,256]{1,0:T(8,128)S(1)}, f32[128,256]{1,0:T(8,128)S(1)}, u32[]{:S(2)}, u32[]{:S(2)}) collective-permute-start(f32[128,256]{1,0:T(8,128)S(1)} %get-tuple-element.83), channel_id=1, source_target_pairs={{0,2},{3,1},{4,6},{7,5},{8,10},{11,9},{12,14},{15,13},{16,18},{19,... | collective-permute-start | bytes 393224 | tf_op jit(solution)/shard_map/ppermute | solution.py:346
  104.6 20.9 %collective-permute-start.22 = (f32[128,768]{1,0:T(8,128)S(1)}, f32[128,768]{1,0:T(8,128)S(1)}, u32[]{:S(2)}, u32[]{:S(2)}) collective-permute-start(f32[128,768]{1,0:T(8,128)S(1)} %get-tuple-element.94), channel_id=1, source_target_pairs={{4,0},{8,4},{12,8},{16,12},{20,16},{24,20},{28,24},{5,1},{9,5},{13... | collective-permute-start | bytes 1179656 | tf_op jit(solution)/shard_map/ppermute | solution.py:366
  113.2 15.9 %collective-permute-start.3 = (f32[128,768]{1,0:T(8,128)S(1)}, f32[128,768]{1,0:T(8,128)S(1)}, u32[]{:S(2)}, u32[]{:S(2)}) collective-permute-start(f32[128,768]{1,0:T(8,128)S(1)} %get-tuple-element.65), channel_id=1, source_target_pairs={{0,4},{4,8},{8,12},{12,16},{16,20},{20,24},{24,28},{1,5},{5,9},{9,... | collective-permute-start | bytes 1179656 | tf_op jit(solution)/shard_map/ppermute | solution.py:366
  116.2 17.7 %collective-permute-start.4 = (f32[128,768]{1,0:T(8,128)S(1)}, f32[128,768]{1,0:T(8,128)S(1)}, u32[]{:S(2)}, u32[]{:S(2)}) collective-permute-start(f32[128,768]{1,0:T(8,128)S(1)} %get-tuple-element.66), channel_id=1, source_target_pairs={{4,0},{8,4},{12,8},{16,12},{20,16},{24,20},{28,24},{5,1},{9,5},{13... | collective-permute-start | bytes 1179656 | tf_op jit(solution)/shard_map/ppermute | solution.py:366
  118.2 0.8 collective-permute-start.12
  118.9 35.8 %collective-permute-start.8 = (f32[128,512]{1,0:T(8,128)S(1)}, f32[128,512]{1,0:T(8,128)S(1)}, u32[]{:S(2)}, u32[]{:S(2)}) collective-permute-start(f32[128,512]{1,0:T(8,128)S(1)} %get-tuple-element.76), channel_id=1, source_target_pairs={{0,4},{4,8},{8,12},{12,16},{16,20},{20,24},{24,28},{1,5},{5,9},{9,... | collective-permute-start | bytes 786440 | tf_op jit(solution)/shard_map/ppermute | solution.py:366
  123.5 35.8 %collective-permute-start.9 = (f32[128,512]{1,0:T(8,128)S(1)}, f32[128,512]{1,0:T(8,128)S(1)}, u32[]{:S(2)}, u32[]{:S(2)}) collective-permute-start(f32[128,512]{1,0:T(8,128)S(1)} %get-tuple-element.77), channel_id=1, source_target_pairs={{4,0},{8,4},{12,8},{16,12},{20,16},{24,20},{28,24},{5,1},{9,5},{13... | collective-permute-start | bytes 786440 | tf_op jit(solution)/shard_map/ppermute | solution.py:366
  125.5 38.6 %collective-permute-start.15 = (f32[128,256]{1,0:T(8,128)S(1)}, f32[128,256]{1,0:T(8,128)S(1)}, u32[]{:S(2)}, u32[]{:S(2)}) collective-permute-start(f32[128,256]{1,0:T(8,128)S(1)} %get-tuple-element.84), channel_id=1, source_target_pairs={{1,2},{2,1},{5,6},{6,5},{9,10},{10,9},{13,14},{14,13},{17,18},{18,... | collective-permute-start | bytes 393224 | tf_op jit(solution)/shard_map/ppermute | solution.py:351
  129.1 35.0 %collective-permute-start.16 = (f32[128,256]{1,0:T(8,128)S(1)}, f32[128,256]{1,0:T(8,128)S(1)}, u32[]{:S(2)}, u32[]{:S(2)}) collective-permute-start(f32[128,256]{1,0:T(8,128)S(1)} %get-tuple-element.85), channel_id=1, source_target_pairs={{0,4},{4,8},{8,12},{12,16},{16,20},{20,24},{24,28},{1,5},{5,9},{9,... | collective-permute-start | bytes 393224 | tf_op jit(solution)/shard_map/ppermute | solution.py:366
  133.9 30.2 %collective-permute-start.17 = (f32[128,256]{1,0:T(8,128)S(1)}, f32[128,256]{1,0:T(8,128)S(1)}, u32[]{:S(2)}, u32[]{:S(2)}) collective-permute-start(f32[128,256]{1,0:T(8,128)S(1)} %get-tuple-element.86), channel_id=1, source_target_pairs={{4,0},{8,4},{12,8},{16,12},{20,16},{24,20},{28,24},{5,1},{9,5},{13... | collective-permute-start | bytes 393224 | tf_op jit(solution)/shard_map/ppermute | solution.py:366
  154.7 19.9 %collective-permute-start.23 = (f32[8,1024]{1,0:T(8,128)S(1)}, f32[8,1024]{1,0:T(8,128)S(1)}, u32[]{:S(2)}, u32[]{:S(2)}) collective-permute-start(f32[8,1024]{1,0:T(8,128)S(1)} %get-tuple-element.105), channel_id=1, source_target_pairs={{0,4},{4,8},{8,12},{12,16},{16,20},{20,24},{24,28},{1,5},{5,9},{9,... | collective-permute-start | bytes 98312 | tf_op jit(solution)/shard_map/ppermute | solution.py:426
  159.3 15.3 %collective-permute-start.24 = (f32[8,1024]{1,0:T(8,128)S(1)}, f32[8,1024]{1,0:T(8,128)S(1)}, u32[]{:S(2)}, u32[]{:S(2)}) collective-permute-start(f32[8,1024]{1,0:T(8,128)S(1)} %get-tuple-element.106), channel_id=1, source_target_pairs={{4,0},{8,4},{12,8},{16,12},{20,16},{24,20},{28,24},{5,1},{9,5},{13... | collective-permute-start | bytes 98312 | tf_op jit(solution)/shard_map/ppermute | solution.py:426
  168.1 27.8 %collective-permute-start.27 = (f32[8,1024]{1,0:T(8,128)S(1)}, f32[8,1024]{1,0:T(8,128)S(1)}, u32[]{:S(2)}, u32[]{:S(2)}) collective-permute-start(f32[8,1024]{1,0:T(8,128)S(1)} %get-tuple-element.113), channel_id=1, source_target_pairs={{0,4},{4,8},{8,12},{12,16},{16,20},{20,24},{24,28},{1,5},{5,9},{9,... | collective-permute-start | bytes 98312 | tf_op jit(solution)/shard_map/ppermute | solution.py:426
  172.7 23.2 %collective-permute-start.28 = (f32[8,1024]{1,0:T(8,128)S(1)}, f32[8,1024]{1,0:T(8,128)S(1)}, u32[]{:S(2)}, u32[]{:S(2)}) collective-permute-start(f32[8,1024]{1,0:T(8,128)S(1)} %get-tuple-element.114), channel_id=1, source_target_pairs={{4,0},{8,4},{12,8},{16,12},{20,16},{24,20},{28,24},{5,1},{9,5},{13... | collective-permute-start | bytes 98312 | tf_op jit(solution)/shard_map/ppermute | solution.py:426
  174.6 8.3 %collective-permute-start.25 = (f32[1,768]{1,0:T(1,128)S(1)}, f32[1,768]{1,0:T(1,128)S(1)}, u32[]{:S(2)}, u32[]{:S(2)}) collective-permute-start(f32[1,768]{1,0:T(1,128)S(1)} %get-tuple-element.107), channel_id=1, source_target_pairs={{0,1},{1,2},{2,3},{4,5},{5,6},{6,7},{8,9},{9,10},{10,11},{12,13},{... | collective-permute-start | bytes 9224 | tf_op jit(solution)/shard_map/ppermute | solution.py:456
  176.6 7.0 %collective-permute-start.26 = (f32[1,768]{1,0:T(1,128)S(1)}, f32[1,768]{1,0:T(1,128)S(1)}, u32[]{:S(2)}, u32[]{:S(2)}) collective-permute-start(f32[1,768]{1,0:T(1,128)S(1)} %get-tuple-element.108), channel_id=1, source_target_pairs={{1,0},{2,1},{3,2},{5,4},{6,5},{7,6},{9,8},{10,9},{11,10},{13,12},{... | collective-permute-start | bytes 9224 | tf_op jit(solution)/shard_map/ppermute | solution.py:456
where the time goes:
time: 201 us; the launch traced here: 197 us
  starting transfers between devices  88.2 us (44%)
  waiting for transfers between devices  65.4 us (33%)
  Pallas kernels  38.7 us (19%)
  between operations  2.59 us (1%)
  local copies, waits for them, and re-layouts  2.21 us (1%)
    ppermute x12, waiting for transfers between devices, on_device(): lax.ppermute(blocks[k], 'col', [p for p in pairs if p[0] in outer] if lat...  64.2 us
    ppermute x8, starting transfers between devices, margins_of(): return (lax.ppermute(last, 'band', up), lax.ppermute(first, 'band', down))  35 us
    ppermute x12, starting transfers between devices, on_device(): lax.ppermute(blocks[k], 'col', [p for p in pairs if p[0] in outer] if lat...  20.7 us
    pallas_call x4, Pallas kernels, run_tile(): pl.pallas_call(functools.partial(tile_kernel, n, margin, t, tuple(parts),...  19 us
    ppermute x4, starting transfers between devices, exchange_rows(): return (lax.ppermute(tails, 'band', up), lax.ppermute(heads, 'band', down))  12.9 us
    pallas_call x2, Pallas kernels, run_horn(): pl.pallas_call(functools.partial(horn_kernel, count, tuple(ranges), tuple...  12.3 us
    ppermute x3, starting transfers between devices, on_device(): rest.insert(0, lax.ppermute(blocks[k], 'col', others))  12.1 us
    pallas_call x2, Pallas kernels, pad_interp(): pl.pallas_call(kernel, out_shape=(VMEM(shape, jnp.bfloat16),) * 2, in_spe...  5.86 us
  transfers between devices with their start and end apart: 29, of which 8 were waited for; matrix products, arithmetic and copies ran while one was open for 0% of the time, Pallas kernels for 19%

commit v1 on v0

v1 whole, which is shorter than its diff:
```python
import functools

import jax
import jax.numpy as jnp
from jax import lax
from jax.experimental import pallas as pl
from jax.experimental.pallas import tpu as pltpu
from jax.sharding import PartitionSpec as P


MARGIN = 128


VMEM = pltpu.VMEM
SMEM = pltpu.SMEM


def split(x):
    high = x.astype(jnp.bfloat16)
    return high, (x - high.astype(jnp.float32)).astype(jnp.bfloat16)


def dot3(a, b):
    (ah, al), (bh, bl) = a, b
    dot = functools.partial(jnp.dot, preferred_element_type=jnp.float32)
    return dot(ah, bh) + (dot(ah, bl) + dot(al, bh))


def params(mib):
    return pltpu.CompilerParams(vmem_limit_bytes=mib << 20)


def shifted_rows_kernel(start, x_ref, high_ref, low_ref):
    width = high_ref.shape[1]
    x = x_ref[0]
    x = jnp.concatenate([x, jnp.zeros((x.shape[0], width - x.shape[1]), x.dtype)], 1)
    high_ref[...], low_ref[...] = split(pltpu.roll(x, start[0], 1))


def shifted_cols_kernel(start, x_ref, high_ref, low_ref):
    count, depth, tile = high_ref.shape
    for t in range(count):
        x = x_ref[t]
        x = jnp.concatenate([x, jnp.zeros((depth - x.shape[0], tile), x.dtype)], 0)
        high_ref[t], low_ref[t] = split(pltpu.roll(x, start[t], 0))


def pad_interp(kernel, start, x, shape):
    return pl.pallas_call(
        kernel,
        out_shape=(VMEM(shape, jnp.bfloat16),) * 2,
        in_specs=[pl.BlockSpec(memory_space=SMEM), pl.BlockSpec(memory_space=VMEM)],
        out_specs=(pl.BlockSpec(memory_space=VMEM),) * 2,
        compiler_params=params(16),
    )(start, x)


def peer(i, k, n):
    return i ^ k if n & (n - 1) == 0 else (i + k) % n


def source(i, k, n):
    return i ^ k if n & (n - 1) == 0 else (i + n - k) % n


def pack_kernel(n, jobs, bands, *outs):
    me = lax.axis_index("col")
    total = bands.shape[1]
    for (k, first), out in zip(jobs, outs):
        wide = out.shape[1]
        start = jnp.clip(peer(me, k, n) * (total // n) + first, 0, total - wide)
        out[...] = bands[:, pl.ds(pl.multiple_of(start, 128), wide)]


def is_even():
    return lax.axis_index("band") % 2 == 0


def select_kernel(n, margin, extra, *refs):
    slots, refs = refs[:n], refs[n:]
    edges, outs = refs[:extra], refs[extra:]
    me = lax.axis_index("col")
    even = is_even()
    rows = slots[0].shape[0]
    part = min(rows, margin)
    many = margin // part

    def fill(out, to_next):
        first, inner = (n - many, rows - part) if to_next else (0, 0)
        for j in range(many):
            for k in range(n):

                @pl.when(source(me, k, n) == first + j)
                def _():
                    out[j * part : (j + 1) * part, :] = slots[k][inner : inner + part, :]

        for j, edge in enumerate(edges):
            row = 15 if to_next else 0
            out[margin + 8 * j : margin + 8 * j + 8, : edge.shape[1]] = jnp.broadcast_to(
                edge[row : row + 1, :], (8, edge.shape[1])
            )

    for which, out in enumerate(outs):
        pl.when(even == (which == 0))(functools.partial(fill, out, True))
        pl.when(even != (which == 0))(functools.partial(fill, out, False))


def margin_rows(first, second, margin, depth, high, low):
    even = is_even().astype(jnp.int32)
    far = depth - margin
    for x, at in ((first, even * far), (second, (1 - even) * far)):
        spot = pl.ds(pl.multiple_of(at, margin), margin)
        high[spot, :], low[spot, :] = split(x[:margin, :])


def edges_of(z):
    return jnp.concatenate([z[:8], z[z.shape[0] - 8 :]], 0)


def tile_kernel(n, margin, t, side, *refs):
    slots, refs = refs[:n], refs[n:]
    first, second, rh, rl, ch, cl = refs[:6]
    refs = refs[6:]
    z, edges, out_h, out_l, line, high, low = refs[side:]
    me = lax.axis_index("col")
    rows = slots[0].shape[0]
    depth = high.shape[0]
    margin_rows(first, second, margin, depth, high, low)
    for k, slot in enumerate(slots):
        spot = pl.ds(pl.multiple_of(margin + source(me, k, n) * rows, rows), rows)
        high[spot, :], low[spot, :] = split(slot[...])
    rr = dot3((rh[...], rl[...]), (high[...], low[...]))
    none = jnp.zeros((rr.shape[0], margin), rr.dtype)
    if side == 0:
        rr = jnp.where(me == 0, jnp.concatenate([none, rr[:, :-margin]], 1), rr)
    else:
        rr = jnp.where(me == n - 1, jnp.concatenate([rr[:, margin:], none], 1), rr)
    new = split(rr)
    out_h[...], out_l[...] = new
    value = dot3(new, (ch[t], cl[t]))
    z[...] = value
    edges[...] = edges_of(value)
    if side == 0:
        line[...] = value[:, :128].T[:8]
    else:
        line[...] = value[:, value.shape[1] - 128 :].T[120:]
        line[0:1, :] = refs[0][0:1, :]


def inner_partial_kernel(n, margin, spans, *refs):
    slots, refs = refs[:n], refs[n:]
    first, second, rh, rl, ch, cl, ah, al, bh, bl, rr = refs[:11]
    zs, (high, low) = refs[11:-2], refs[-2:]
    me = lax.axis_index("col")
    rows = slots[0].shape[0]
    depth = high.shape[0]
    half = depth // 2
    many = max(margin // rows, 1)
    margin_rows(first, second, margin, depth, high, low)
    for k, slot in enumerate(slots):
        own = source(me, k, n)
        at = jnp.where(own < many, margin + own * rows, depth - margin - (n - own) * rows)

        @pl.when((own < many) | (own >= n - many))
        def _():
            spot = pl.ds(pl.multiple_of(at, rows), rows)
            high[spot, :], low[spot, :] = split(slot[...])

    pick = lambda v: jnp.concatenate([v[:, :half], v[:, v.shape[1] - half :]], 1)
    rr[...] = dot3((pick(rh[...]), pick(rl[...])), (high[...], low[...]))
    for (t, before, fresh, after), z in zip(spans, zs):
        total = jnp.zeros(z.shape, jnp.float32)
        if before:
            wide = ah.shape[1]
            left = (ah[:, wide - before :], al[:, wide - before :])
            total = total + dot3(left, (ch[t, :before, :], cl[t, :before, :]))
        if after:
            right = (bh[:, :after], bl[:, :after])
            total = total + dot3(right, (ch[t, before + fresh :, :], cl[t, before + fresh :, :]))
        z[...] = total


def inner_kernel(n, margin, spans, *refs):
    slots, refs = refs[:n], refs[n:]
    rh, rl, ch, cl, rr, line_a, line_b = refs[:7]
    refs = refs[7:]
    count = len(spans)
    parts, zs, (edges, high, low) = refs[:count], refs[count : 2 * count], refs[2 * count :]
    me = lax.axis_index("col")
    rows = slots[0].shape[0]
    inner = high.shape[0]
    depth = rh.shape[1]
    many = max(margin // rows, 1)
    for k, slot in enumerate(slots):
        own = source(me, k, n)

        @pl.when((own >= many) & (own < n - many))
        def _():
            spot = pl.ds(pl.multiple_of((own - many) * rows, rows), rows)
            high[spot, :], low[spot, :] = split(slot[...])

    low_k = (depth - inner) // 2
    cols = slice(low_k, low_k + inner)
    new = split(rr[...] + dot3((rh[:, cols], rl[:, cols]), (high[...], low[...])))
    tile = zs[0].shape[1]
    for j, ((t, before, fresh, after), part, z) in enumerate(zip(spans, parts, zs)):
        at = max(j * tile - 2 * margin, 0)
        window = tuple(v[:, at : at + fresh] for v in new)
        c = (ch[t, before : before + fresh, :], cl[t, before : before + fresh, :])
        value = part[...] + dot3(window, c)
        z[...] = value
        edges[:, j * tile : (j + 1) * tile] = edges_of(value)
    even = me % 2 == 0
    left = jnp.where(even, line_b[7:8, :], line_a[7:8, :])
    right = jnp.where(even, line_a[0:1, :], line_b[0:1, :])
    wide = count * tile
    for j, v in enumerate((left, right)):
        at = wide + 128 * j
        edges[:8, at : at + 128] = jnp.broadcast_to(v[:, :128], (8, 128))
        edges[8:, at : at + 128] = jnp.broadcast_to(v[:, tile - 128 :], (8, 128))


def across(z):
    width = z.shape[1]
    here = z[:, 128 : width - 128]
    before = pltpu.roll(z, 1, 1)[:, 128 : width - 128]
    after = pltpu.roll(z, width - 1, 1)[:, 128 : width - 128]
    return after - before, before + 2.0 * here + after


def maps_of(p, q, scale):
    p = p * scale
    q = q * scale
    total = p * p + q * q
    inv = lax.rsqrt(1.0 + total)
    root = total * lax.rsqrt(jnp.maximum(total, 1.2e-38))
    return root * inv, (0.70710678 - 0.5 * p + 0.5 * q) * inv


def upright(line, rows):
    return jnp.broadcast_to(line, (128, rows)).T


def cut(tiles, rows, first, last, ends):
    tile = tiles[0].shape[1]
    width = tile * len(tiles)
    pieces = [ends[0]] if first < 0 else []
    at = max(first, 0)
    while at < min(last, width):
        t, stop = at // tile, min(at // tile * tile + tile, last)
        pieces.append(tiles[t][rows, at - t * tile : stop - t * tile])
        at = stop
    if last > width:
        pieces.append(ends[1])
    return jnp.concatenate(pieces, 1)


def horn_kernel(count, ranges, fresh, held, spacing, *refs):
    tiles, (line_a, line_b) = refs[:count], refs[count : count + 2]
    elev, slope, shade, *bufs, l_col, r_col, sem_z, sem_out = refs[count + 2 + held :]
    tile = tiles[0].shape[0]
    width = tile * count
    blocks = 4 if tile % 32 == 0 else 1
    rows = tile // blocks

    def keep(j):
        return pltpu.make_async_copy(
            tiles[fresh[j]], elev.at[:, pl.ds(fresh[j] * tile, tile)], sem_z.at[j]
        )

    def store(i, b, which):
        first, last = ranges[i]
        return pltpu.make_async_copy(
            bufs[2 * i + which].at[pl.ds(b * rows, rows), :],
            (slope, shade)[which].at[pl.ds(b * rows, rows), pl.ds(first, last - first)],
            sem_out.at[i, b, which],
        )

    for j in range(len(fresh)):
        keep(j).start()
    even = lax.axis_index("col") % 2 == 0
    if any(first == 0 for first, _ in ranges):
        l_col[...] = upright(jnp.where(even, line_b[7:8, :], line_a[7:8, :]), tile)
    if any(last == width for _, last in ranges):
        r_col[...] = upright(jnp.where(even, line_a[0:1, :], line_b[0:1, :]), tile)
    strips = tile // 8
    for i, (first, last) in enumerate(ranges):
        pieces, at = [], first
        while at < last:
            pieces.append((at, min(at + 384, last)))
            at = pieces[-1][1]
        for b in range(blocks):
            for lo, hi in pieces:
                row = lax.broadcasted_iota(jnp.int32, (8, hi - lo), 0)
                scale = 0.125 / jnp.full((8, hi - lo), spacing[0])

                def load(g):
                    spot = pl.ds(pl.multiple_of(g * 8, 8), 8)
                    ends = (l_col[spot, :], r_col[spot, :])
                    return across(cut(tiles, spot, lo - 128, hi + 128, ends))

                def rolled(v):
                    return pltpu.roll(v, 1, 0), pltpu.roll(v, 7, 0)

                def strip(r, carry):
                    g = b * (rows // 8) + r
                    e, e1, e7, f1, f7, e1_above, f1_above = carry
                    e_next, f_next = load(jnp.minimum(g + 1, strips - 1))
                    e1_next, e7_next = rolled(e_next)
                    f1_next, f7_next = rolled(f_next)
                    e_up = jnp.where(row == 0, e1_above, e1)
                    f_up = jnp.where(row == 0, f1_above, f1)
                    e_down = jnp.where(row == 7, e7_next, e7)
                    f_down = jnp.where(row == 7, f7_next, f7)
                    spot = pl.ds(pl.multiple_of(g * 8, 8), 8)
                    where = pl.ds(lo - first, hi - lo)
                    bufs[2 * i][spot, where], bufs[2 * i + 1][spot, where] = maps_of(
                        e_up + 2.0 * e + e_down, f_down - f_up, scale
                    )
                    return e_next, e1_next, e7_next, f1_next, f7_next, e1, f1

                g0 = b * (rows // 8)
                e_above, f_above = load(max(g0 - 1, 0))
                e, f = load(g0)
                start = (e, *rolled(e), *rolled(f), rolled(e_above)[0], rolled(f_above)[0])
                lax.fori_loop(0, rows // 8, strip, start, unroll=8)
            store(i, b, 0).start()
            store(i, b, 1).start()
    for i in range(len(ranges)):
        for b in range(blocks):
            store(i, b, 0).wait()
            store(i, b, 1).wait()
    for j in range(len(fresh)):
        keep(j).wait()


def border_kernel(count, margin, spacing, *refs):
    tiles, refs = refs[:count], refs[count:]
    line_a, line_b, outer_a, outer_b, inner_a, inner_b = refs[:6]
    slope, shade, buf, sem = refs[-4:]
    tile = tiles[0].shape[0]
    width = tile * count
    middle = width - 2 * tile
    even = is_even()
    side = lax.axis_index("col") % 2 == 0
    left = jnp.where(side, line_b[7:8, :], line_a[7:8, :])
    right = jnp.where(side, line_a[0:1, :], line_b[0:1, :])
    row = lax.broadcasted_iota(jnp.int32, (8, width), 0)
    scale = 0.125 / jnp.full((8, width), spacing[0])

    def halo(above):
        pick = lambda a, b: jnp.where(even, b, a) if above else jnp.where(even, a, b)
        outer = [
            pick(*(v[margin + 8 * j : margin + 8 * j + 1, :tile] for v in (outer_a, outer_b)))
            for j in range(2)
        ]
        at = 15 if above else 0
        inner = pick(inner_a[at : at + 1, :], inner_b[at : at + 1, :])
        ends = [inner[:, middle : middle + 128], inner[:, middle + 128 :]]
        ends = [jnp.broadcast_to(v, (8, 128)) for v in ends]
        j = 1 if above else 0
        ends[j] = pltpu.roll(ends[j], 1 if above else 127, 1)
        values = jnp.concatenate([outer[0], inner[:, :middle], outer[1]], 1)
        values = jnp.broadcast_to(values, (8, width))
        return across(jnp.concatenate([ends[0], values, ends[1]], 1))

    def strip(at):
        lane = at // 128 * 128
        ends = [upright(v[:, lane : lane + 128], 128)[at - lane : at - lane + 8] for v in (left, right)]
        return across(cut(tiles, slice(at, at + 8), -128, width + 128, ends))

    copies = []
    for where, at in enumerate((0, tile - 8)):
        e, f = strip(at)
        above = halo(True) if where == 0 else [pltpu.roll(v, 1, 0) for v in strip(at - 8)]
        below = halo(False) if where == 1 else [pltpu.roll(v, 7, 0) for v in strip(8)]
        e_up, f_up = [jnp.where(row == 0, a, pltpu.roll(v, 1, 0)) for a, v in zip(above, (e, f))]
        e_down, f_down = [jnp.where(row == 7, a, pltpu.roll(v, 7, 0)) for a, v in zip(below, (e, f))]
        found = maps_of(e_up + 2.0 * e + e_down, f_down - f_up, scale)
        for j, (v, out) in enumerate(zip(found, (slope, shade))):
            buf[where, j] = v
            copies.append(
                pltpu.make_async_copy(buf.at[where, j], out.at[pl.ds(at, 8), :], sem.at[where, j])
            )
            copies[-1].start()
    for copy in copies:
        copy.wait()


def partners(count):
    found = []
    for start in (0, 1):
        pairs = [(i, i + 1) for i in range(start, count - 1, 2)]
        found.append(pairs + [(j, i) for i, j in pairs])
    return found


def on_device(bands, row_interp, col_interp, row_start, col_start, spacing):
    n = lax.axis_size("col")
    nb = lax.axis_size("band")
    margin = MARGIN
    rows, total = bands.shape
    width = total // n
    tile = row_interp.shape[1]
    count = col_interp.shape[0]
    depth = tile + 2 * margin
    f32, bf16 = jnp.float32, jnp.bfloat16
    vm = pl.BlockSpec(memory_space=VMEM)
    sm = pl.BlockSpec(memory_space=SMEM)
    hbm = pl.BlockSpec(memory_space=pltpu.HBM)

    def call(kernel, outs, operands, mib, scratch=()):
        return pl.pallas_call(
            kernel,
            out_shape=tuple(VMEM(shape, dtype) for shape, dtype in outs),
            in_specs=[vm] * len(operands),
            out_specs=(vm,) * len(outs),
            scratch_shapes=scratch,
            compiler_params=params(mib),
        )(*operands)

    def exchange(axis, size, first, second):
        a, b = partners(size)
        return lax.ppermute(first, axis, a), lax.ppermute(second, axis, b)

    chunks = [(-margin, tile + margin), (width - tile - margin, width + margin)]
    chunks.append((tile + margin, width - tile - margin))
    many = max(margin // rows, 1)
    outer = [s for s in range(n) if s < many or s >= n - many]

    def pack(jobs):
        return call(
            functools.partial(pack_kernel, n, tuple((k, chunk[0]) for k, chunk in jobs)),
            [((rows, chunk[1] - chunk[0]), f32) for _, chunk in jobs],
            [bands],
            8,
        )

    blocks = [[None, *pack([(k, chunks[0]) for k in range(1, n)])]]
    packed = pack([(0, chunks[0])] + [(k, chunk) for chunk in chunks[1:] for k in range(n)])
    blocks[0][0] = packed[0]
    blocks += [list(packed[1 : n + 1]), list(packed[n + 1 :])]

    def send(got, keep):
        found = [got[0]]
        for k in range(1, n):
            pairs = [(i, peer(i, k, n)) for i in range(n) if keep(i)]
            found.append(lax.ppermute(got[k], "col", pairs))
        return found

    slots = [send(blocks[i], lambda i: True) for i in range(2)]
    slots.append(send(blocks[2], lambda i: i in outer))
    slots.append(send(blocks[2], lambda i: i not in outer))

    rh, rl = pad_interp(shifted_rows_kernel, row_start, row_interp, (tile, depth))
    ch, cl = pad_interp(shifted_cols_kernel, col_start, col_interp, (count, depth, tile))

    def margins_of(index, edges):
        got = slots[index]
        shape = (margin + 8 * len(edges), got[0].shape[1])
        sent = call(
            functools.partial(select_kernel, n, margin, len(edges)),
            [(shape, f32)] * 2,
            [*got, *edges],
            8,
        )
        return exchange("band", nb, *sent)

    tiles, edges, rr, line = [None] * count, [], [], []
    for side, t in enumerate((0, count - 1)):
        margins = margins_of(side, [])
        wide = chunks[side][1] - chunks[side][0]
        z, edge, high, low, lines = call(
            functools.partial(tile_kernel, n, margin, t, side),
            [((tile, tile), f32), ((16, tile), f32)]
            + [((tile, wide), bf16)] * 2
            + [((8, tile), f32)],
            [*slots[side], *margins, rh, rl, ch, cl, *line],
            16,
            [VMEM((depth, wide), bf16)] * 2,
        )
        tiles[t] = z
        edges.append(edge)
        rr += [high, low]
        line = [lines]
    lines = exchange("col", n, line[0], line[0])

    def run_horn(ranges, fresh, held):
        shown = [tiles[0] if v is None else v for v in tiles]
        scratch = [VMEM((tile, last - first), f32) for first, last in ranges for _ in range(2)]
        return pl.pallas_call(
            functools.partial(horn_kernel, count, tuple(ranges), tuple(fresh), len(held)),
            out_shape=(jax.ShapeDtypeStruct((tile, width), f32),) * 3,
            in_specs=[sm] + [vm] * (count + 2) + [hbm] * len(held),
            out_specs=(hbm,) * 3,
            scratch_shapes=scratch
            + [VMEM((tile, 128), f32)] * 2
            + [
                pltpu.SemaphoreType.DMA((len(fresh),)),
                pltpu.SemaphoreType.DMA((len(ranges), 4, 2)),
            ],
            input_output_aliases={count + 3 + j: j for j in range(len(held))},
            compiler_params=params(16),
        )(spacing, *shown, *lines, *held)

    margins = margins_of(2, edges)
    maps = run_horn([(0, tile - 128), (width - tile + 128, width)], [0, count - 1], [])

    spans = []
    for t in range(1, count - 1):
        low, high = t * tile - margin, (t + 1) * tile + margin
        before, after = max(chunks[2][0] - low, 0), max(high - chunks[2][1], 0)
        spans.append((t, before, depth - before - after, after))
    wide = chunks[2][1] - chunks[2][0]
    part, *partial = call(
        functools.partial(inner_partial_kernel, n, margin, tuple(spans)),
        [((tile, wide), f32)] + [((tile, tile), f32)] * len(spans),
        [*slots[2], *margins, rh, rl, ch, cl, *rr],
        16,
        [VMEM((2 * margin + len(outer) * rows, wide), bf16)] * 2,
    )
    *found, edge = call(
        functools.partial(inner_kernel, n, margin, tuple(spans)),
        [((tile, tile), f32)] * len(spans) + [((16, len(spans) * tile + 256), f32)],
        [*slots[3], rh, rl, ch, cl, part, *lines, *partial],
        16,
        [VMEM(((n - len(outer)) * rows, wide), bf16)] * 2,
    )
    for (t, *_), z in zip(spans, found):
        tiles[t] = z
    ends = exchange("band", nb, edge, edge)
    elev, *maps = run_horn([(tile - 128, width - tile + 128)], [t for t, *_ in spans], list(maps))
    slope, shade = pl.pallas_call(
        functools.partial(border_kernel, count, margin),
        out_shape=(jax.ShapeDtypeStruct((tile, width), f32),) * 2,
        in_specs=[sm] + [vm] * (count + 6) + [hbm] * 2,
        out_specs=(hbm,) * 2,
        scratch_shapes=[VMEM((2, 2, 8, width), f32), pltpu.SemaphoreType.DMA((2, 2))],
        input_output_aliases={count + 7: 0, count + 8: 1},
        compiler_params=params(8),
        name="border",
    )(spacing, *tiles, *lines, *margins, *ends, *maps)
    return (elev, slope, shade)


def solution(mesh):
    in_specs = (
        P(("band", "col"), None),
        P("band", None, None),
        P("col", None, None),
        P("band"),
        P("col"),
        P("band"),
    )
    out_specs = (P("band", "col"), P("band", "col"), P("band", "col"))

    return jax.shard_map(
        on_device, mesh=mesh, in_specs=in_specs, out_specs=out_specs, check_vma=False
    )
```

time: 201 us -> 152 us (0.76); the launches traced: 197 us -> 151 us
  starting transfers between devices: 88.2 us -> 62.2 us
  waiting for transfers between devices: 65.4 us -> 47.1 us
    ppermute x29 -> x22, starting transfers between devices: 88.2 us -> 62.2 us  [the longest x10 38.4 us: exchange(): return (lax.ppermute(first, axis, a), lax.ppermute(second, axis, b))]
    ppermute x29 -> x22, waiting for transfers between devices: 65.4 us -> 47.1 us  [the longest x12 46.9 us: send(): found.append(lax.ppermute(got[k], 'col', pairs))]
    pallas_call x12 -> x10, Pallas kernels: 20.6 us -> 18.8 us  [the longest x9 17.6 us: call(): pl.pallas_call(kernel, out_shape=tuple((VMEM(shape, dtype) for shape, dty...]
  transfers between devices with their start and end apart: 29 -> 22, of which waited for: 8 -> 7; matrix products, arithmetic and copies ran while one was open for 0% -> 0% of each run, Pallas kernels for 19% -> 22%
where the time goes in v1:
time: 152 us; the launch traced here: 151 us
  starting transfers between devices  62.2 us (41%)
  waiting for transfers between devices  47.1 us (31%)
  Pallas kernels  37.5 us (25%)
  between operations  2.47 us (2%)
  local copies, waits for them, and re-layouts  2.2 us (1%)
    ppermute x12, waiting for transfers between devices, send(): found.append(lax.ppermute(got[k], 'col', pairs))  46.9 us
    ppermute x10, starting transfers between devices, exchange(): return (lax.ppermute(first, axis, a), lax.ppermute(second, axis, b))  38.4 us
    ppermute x12, starting transfers between devices, send(): found.append(lax.ppermute(got[k], 'col', pairs))  23.8 us
    pallas_call x9, Pallas kernels, call(): pl.pallas_call(kernel, out_shape=tuple((VMEM(shape, dtype) for shape, dty...  17.6 us
    pallas_call x2, Pallas kernels, run_horn(): pl.pallas_call(functools.partial(horn_kernel, count, tuple(ranges), tuple...  12.8 us
    pallas_call x2, Pallas kernels, pad_interp(): pl.pallas_call(kernel, out_shape=(VMEM(shape, jnp.bfloat16),) * 2, in_spe...  5.85 us
  transfers between devices with their start and end apart: 22, of which 7 were waited for; matrix products, arithmetic and copies ran while one was open for 0% of the time, Pallas kernels for 22%

profile of v1, /device:TPU:11, one launch (start us, length us, event | category | flops | bytes accessed | tf_op | source)
XLA Modules:
  0.0 151.4 jit_solution(8061084055189174216)
XLA Ops:
  0.6 2.2 %copy-done = f32[128,8192]{1,0:T(8,128)S(1)} copy-done((f32[128,8192]{1,0:T(8,128)S(1)}, f32[128,8192]{1,0:T(8,128)}, u32[]{:S(2)}) %copy-start) | copy-done | bytes 4194328
  2.8 0.1 shard_map.86
  2.9 0.0 copy-start.1
  2.9 0.2 collective-permute-start
  3.1 2.3 %collective-permute-start.1 = (f32[128,768]{1,0:T(8,128)S(1)}, f32[128,768]{1,0:T(8,128)S(1)}, u32[]{:S(2)}, u32[]{:S(2)}) collective-permute-start(f32[128,768]{1,0:T(8,128)S(1)} %get-tuple-element.51), channel_id=1, source_target_pairs={{0,2},{1,3},{2,0},{3,1},{4,6},{5,7},{6,4},{7,5},{8,10},{9,11},{10,... | collective-permute-start | bytes 1179656 | tf_op jit(solution)/shard_map/ppermute | solution.py:448
  5.5 0.2 collective-permute-start.2
  5.6 0.2 shard_map.85
  5.9 1.2 collective-permute-start.11
  7.1 2.2 %collective-permute-start.12 = (f32[128,768]{1,0:T(8,128)S(1)}, f32[128,768]{1,0:T(8,128)S(1)}, u32[]{:S(2)}, u32[]{:S(2)}) collective-permute-start(f32[128,768]{1,0:T(8,128)S(1)} %get-tuple-element.67), channel_id=1, source_target_pairs={{0,2},{1,3},{2,0},{3,1},{4,6},{5,7},{6,4},{7,5},{8,10},{9,11},{10,... | collective-permute-start | bytes 1179656 | tf_op jit(solution)/shard_map/ppermute | solution.py:448
  9.2 9.4 %collective-permute-done.refs_1_ = f32[128,768]{1,0:T(8,128)S(1)} collective-permute-done((f32[128,768]{1,0:T(8,128)S(1)}, f32[128,768]{1,0:T(8,128)S(1)}, u32[]{:S(2)}, u32[]{:S(2)}) %collective-permute-start) | collective-permute-done | bytes 393248 | tf_op jit(solution)/shard_map/ppermute | solution.py:448
  18.6 1.9 %collective-permute-start.13 = (f32[128,768]{1,0:T(8,128)S(1)}, f32[128,768]{1,0:T(8,128)S(1)}, u32[]{:S(2)}, u32[]{:S(2)}) collective-permute-start(f32[128,768]{1,0:T(8,128)S(1)} %get-tuple-element.68), channel_id=1, source_target_pairs={{0,3},{1,2},{2,1},{3,0},{4,7},{5,6},{6,5},{7,4},{8,11},{9,10},{10,... | collective-permute-start | bytes 1179656 | tf_op jit(solution)/shard_map/ppermute | solution.py:448
  20.5 2.0 %collective-permute-done.1.refs_2_ = f32[128,768]{1,0:T(8,128)S(1)} collective-permute-done((f32[128,768]{1,0:T(8,128)S(1)}, f32[128,768]{1,0:T(8,128)S(1)}, u32[]{:S(2)}, u32[]{:S(2)}) %collective-permute-start.1) | collective-permute-done | bytes 393248 | tf_op jit(solution)/shard_map/ppermute | solution.py:448
  22.5 16.8 %collective-permute-done.2.refs_3_ = f32[128,768]{1,0:T(8,128)S(1)} collective-permute-done((f32[128,768]{1,0:T(8,128)S(1)}, f32[128,768]{1,0:T(8,128)S(1)}, u32[]{:S(2)}, u32[]{:S(2)}) %collective-permute-start.2) | collective-permute-done | bytes 393248 | tf_op jit(solution)/shard_map/ppermute | solution.py:448
  39.3 0.1 shard_map.87
  39.4 20.0 %collective-permute-start.3 = (f32[128,768]{1,0:T(8,128)S(1)}, f32[128,768]{1,0:T(8,128)S(1)}, u32[]{:S(2)}, u32[]{:S(2)}) collective-permute-start(f32[128,768]{1,0:T(8,128)S(1)} %get-tuple-element.53), channel_id=1, source_target_pairs={{0,4},{8,12},{16,20},{24,28},{4,0},{12,8},{20,16},{28,24},{1,5},{9... | collective-permute-start | bytes 1179656 | tf_op jit(solution)/shard_map/ppermute | solution.py:424
  59.4 3.0 %collective-permute-start.4 = (f32[128,768]{1,0:T(8,128)S(1)}, f32[128,768]{1,0:T(8,128)S(1)}, u32[]{:S(2)}, u32[]{:S(2)}) collective-permute-start(f32[128,768]{1,0:T(8,128)S(1)} %get-tuple-element.54), channel_id=1, source_target_pairs={{4,8},{12,16},{20,24},{8,4},{16,12},{24,20},{5,9},{13,17},{21,25},... | collective-permute-start | bytes 1179656 | tf_op jit(solution)/shard_map/ppermute | solution.py:424
  62.5 0.0 collective-permute-done.11.refs_1_
  62.5 1.3 collective-permute-start.8
  63.8 9.2 %collective-permute-done.13.refs_3_ = f32[128,768]{1,0:T(8,128)S(1)} collective-permute-done((f32[128,768]{1,0:T(8,128)S(1)}, f32[128,768]{1,0:T(8,128)S(1)}, u32[]{:S(2)}, u32[]{:S(2)}) %collective-permute-start.13) | collective-permute-done | bytes 393248 | tf_op jit(solution)/shard_map/ppermute | solution.py:448
  73.0 0.1 shard_map.91
  73.1 1.8 %collective-permute-start.14 = (f32[128,768]{1,0:T(8,128)S(1)}, f32[128,768]{1,0:T(8,128)S(1)}, u32[]{:S(2)}, u32[]{:S(2)}) collective-permute-start(f32[128,768]{1,0:T(8,128)S(1)} %get-tuple-element.69), channel_id=1, source_target_pairs={{0,4},{8,12},{16,20},{24,28},{4,0},{12,8},{20,16},{28,24},{1,5},{9... | collective-permute-start | bytes 1179656 | tf_op jit(solution)/shard_map/ppermute | solution.py:424
  74.9 3.0 %collective-permute-start.15 = (f32[128,768]{1,0:T(8,128)S(1)}, f32[128,768]{1,0:T(8,128)S(1)}, u32[]{:S(2)}, u32[]{:S(2)}) collective-permute-start(f32[128,768]{1,0:T(8,128)S(1)} %get-tuple-element.70), channel_id=1, source_target_pairs={{4,8},{12,16},{20,24},{8,4},{16,12},{24,20},{5,9},{13,17},{21,25},... | collective-permute-start | bytes 1179656 | tf_op jit(solution)/shard_map/ppermute | solution.py:424
  77.9 1.3 collective-permute-start.9
  79.3 0.9 collective-permute-start.10
  80.8 1.1 shard_map.88
  82.0 4.7 %shard_map.89 = (bf16[4,768,512]{2,1,0:T(8,128)(2,1)S(1)}, bf16[4,768,512]{2,1,0:T(8,128)(2,1)S(1)}) custom-call(s32[4]{0:T(128)S(1)} %copy-done.2, f32[4,640,512]{2,1,0:T(8,128)S(1)} %bitcast.1), custom_call_target="tpu_custom_call" | custom-call | tf_op jit(solution)/shard_map/pallas_call | solution.py:49
  86.7 5.8 %shard_map.90 = (f32[512,512]{1,0:T(8,128)S(1)}, f32[16,512]{1,0:T(8,128)S(1)}, bf16[512,768]{1,0:T(8,128)(2,1)S(1)}, bf16[512,768]{1,0:T(8,128)(2,1)S(1)}, f32[8,512]{1,0:T(8,128)S(1)}) custom-call(f32[128,768]{1,0:T(8,128)S(1)} %get-tuple-element.49.refs_0_, f32[128,768]{1,0:T(8,128)S(1)} %collective-permute-done.refs_1_, ...), custom_call_target="tpu_custom_call" | custom-call | tf_op jit(solution)/shard_map/pallas_call | solution.py:413
  92.5 6.2 %shard_map.92 = (f32[512,512]{1,0:T(8,128)S(1)}, f32[16,512]{1,0:T(8,128)S(1)}, bf16[512,768]{1,0:T(8,128)(2,1)S(1)}, bf16[512,768]{1,0:T(8,128)(2,1)S(1)}, f32[8,512]{1,0:T(8,128)S(1)}) custom-call(f32[128,768]{1,0:T(8,128)S(1)} %get-tuple-element.65.refs_0_, f32[128,768]{1,0:T(8,128)S(1)} %collective-permute-done.11.refs_1_, ...), custom_call_target="tpu_custom_call" | custom-call | tf_op jit(solution)/shard_map/pallas_call | solution.py:413
  98.7 0.0 collective-permute-done.8.refs_1_
  98.7 0.0 collective-permute-done.9.refs_2_
  98.7 0.1 shard_map.93
  98.8 0.1 collective-permute-start.16
  98.9 3.5 %collective-permute-start.17 = (f32[144,768]{1,0:T(8,128)S(1)}, f32[144,768]{1,0:T(8,128)S(1)}, u32[]{:S(2)}, u32[]{:S(2)}) collective-permute-start(f32[144,768]{1,0:T(8,128)S(1)} %get-tuple-element.74), channel_id=1, source_target_pairs={{4,8},{12,16},{20,24},{8,4},{16,12},{24,20},{5,9},{13,17},{21,25},... | collective-permute-start | bytes 1327112 | tf_op jit(solution)/shard_map/ppermute | solution.py:424
  102.4 7.8 %collective-permute-start.5 = (f32[128,768]{1,0:T(8,128)S(1)}, f32[128,768]{1,0:T(8,128)S(1)}, u32[]{:S(2)}, u32[]{:S(2)}) collective-permute-start(f32[128,768]{1,0:T(8,128)S(1)} %get-tuple-element.61), channel_id=1, source_target_pairs={{1,0},{2,3},{5,4},{6,7},{9,8},{10,11},{13,12},{14,15},{17,16},{18,... | collective-permute-start | bytes 1179656 | tf_op jit(solution)/shard_map/ppermute | solution.py:448
  110.3 2.3 %collective-permute-start.6 = (f32[128,768]{1,0:T(8,128)S(1)}, f32[128,768]{1,0:T(8,128)S(1)}, u32[]{:S(2)}, u32[]{:S(2)}) collective-permute-start(f32[128,768]{1,0:T(8,128)S(1)} %get-tuple-element.62), channel_id=1, source_target_pairs={{1,3},{2,0},{5,7},{6,4},{9,11},{10,8},{13,15},{14,12},{17,19},{18,... | collective-permute-start | bytes 1179656 | tf_op jit(solution)/shard_map/ppermute | solution.py:448
  112.6 2.2 %collective-permute-start.7 = (f32[128,768]{1,0:T(8,128)S(1)}, f32[128,768]{1,0:T(8,128)S(1)}, u32[]{:S(2)}, u32[]{:S(2)}) collective-permute-start(f32[128,768]{1,0:T(8,128)S(1)} %get-tuple-element.63), channel_id=1, source_target_pairs={{1,2},{2,1},{5,6},{6,5},{9,10},{10,9},{13,14},{14,13},{17,18},{18,... | collective-permute-start | bytes 1179656 | tf_op jit(solution)/shard_map/ppermute | solution.py:448
  114.8 0.1 collective-permute-start.18
  114.9 3.1 %collective-permute-start.19 = (f32[8,512]{1,0:T(8,128)S(1)}, f32[8,512]{1,0:T(8,128)S(1)}, u32[]{:S(2)}, u32[]{:S(2)}) collective-permute-start(f32[8,512]{1,0:T(8,128)S(1)} %get-tuple-element.80), channel_id=1, source_target_pairs={{1,2},{2,1},{5,6},{6,5},{9,10},{10,9},{13,14},{14,13},{17,18},{18,... | collective-permute-start | bytes 49160 | tf_op jit(solution)/shard_map/ppermute | solution.py:424
  118.0 2.5 %shard_map.94 = (f32[512,768]{1,0:T(8,128)S(1)}, f32[512,512]{1,0:T(8,128)S(1)}, f32[512,512]{1,0:T(8,128)S(1)}) custom-call(f32[128,768]{1,0:T(8,128)S(1)} %get-tuple-element.60.refs_0_, f32[128,768]{1,0:T(8,128)S(1)} %collective-permute-done.8.refs_1_, f32[128,768]{1,0:T(8,128)S(1)} %collective-permute-done.9.refs_2_, ...), custom_call_target="tpu_custom_call" | custom-call | tf_op jit(solution)/shard_map/pallas_call | solution.py:413
  120.5 6.3 %collective-permute-done.5.refs_1_ = f32[128,768]{1,0:T(8,128)S(1)} collective-permute-done((f32[128,768]{1,0:T(8,128)S(1)}, f32[128,768]{1,0:T(8,128)S(1)}, u32[]{:S(2)}, u32[]{:S(2)}) %collective-permute-start.5) | collective-permute-done | bytes 393248 | tf_op jit(solution)/shard_map/ppermute | solution.py:448
  126.8 3.1 %collective-permute-done.7.refs_3_ = f32[128,768]{1,0:T(8,128)S(1)} collective-permute-done((f32[128,768]{1,0:T(8,128)S(1)}, f32[128,768]{1,0:T(8,128)S(1)}, u32[]{:S(2)}, u32[]{:S(2)}) %collective-permute-start.7) | collective-permute-done | bytes 393248 | tf_op jit(solution)/shard_map/ppermute | solution.py:448
  129.9 0.2 collective-permute-done.19.refs_10_.refs_5_
  130.1 2.6 %shard_map.95 = (f32[512,512]{1,0:T(8,128)S(1)}, f32[512,512]{1,0:T(8,128)S(1)}, f32[16,1280]{1,0:T(8,128)S(1)}) custom-call(f32[128,768]{1,0:T(8,128)S(1)} %get-tuple-element.60.refs_0_, f32[128,768]{1,0:T(8,128)S(1)} %collective-permute-done.5.refs_1_, f32[128,768]{1,0:T(8,128)S(1)} %collective-permute-done.6.refs_2_, ...), custom_call_target="tpu_custom_call" | custom-call | tf_op jit(solution)/shard_map/pallas_call | solution.py:413
  132.6 0.1 collective-permute-start.20
  132.7 3.8 %collective-permute-start.21 = (f32[16,1280]{1,0:T(8,128)S(1)}, f32[16,1280]{1,0:T(8,128)S(1)}, u32[]{:S(2)}, u32[]{:S(2)}) collective-permute-start(f32[16,1280]{1,0:T(8,128)S(1)} %get-tuple-element.90), channel_id=1, source_target_pairs={{4,8},{12,16},{20,24},{8,4},{16,12},{24,20},{5,9},{13,17},{21,25},... | collective-permute-start | bytes 245768 | tf_op jit(solution)/shard_map/ppermute | solution.py:424
  137.1 4.8 %shard_map.96 = (f32[512,2048]{1,0:T(8,128)}, f32[512,2048]{1,0:T(8,128)}, f32[512,2048]{1,0:T(8,128)}) custom-call(f32[1]{0:T(128)S(6)} %copy.20.spacing, f32[512,512]{1,0:T(8,128)S(1)} %get-tuple-element.59.refs_0_.refs_1_.refs_2_, f32[512,512]{1,0:T(8,128)S(1)} %get-tuple-element.59.refs_0_.refs_1_.refs_2_, ...), custom_call_target="tpu_custom_call" | custom-call | tf_op jit(solution)/shard_map/pallas_call | solution.py:491
  142.0 8.0 %shard_map.97 = (f32[512,2048]{1,0:T(8,128)}, f32[512,2048]{1,0:T(8,128)}, f32[512,2048]{1,0:T(8,128)}) custom-call(f32[1]{0:T(128)S(6)} %copy.20.spacing, f32[512,512]{1,0:T(8,128)S(1)} %get-tuple-element.59.refs_0_.refs_1_.refs_2_, f32[512,512]{1,0:T(8,128)S(1)} %get-tuple-element.83.refs_1_, ...), custom_call_target="tpu_custom_call", output_to_operand_aliasing={{0}: (7, {}), {1}: (8, {}), {2}: (9, {})} | custom-call | tf_op jit(solution)/shard_map/pallas_call | solution.py:491
  150.0 1.2 border.1
  (21 shorter events, 0.0 us)
Async XLA Ops:
  0.6 2.2 %copy-start = (f32[128,8192]{1,0:T(8,128)S(1)}, f32[128,8192]{1,0:T(8,128)}, u32[]{:S(2)}) copy-start(f32[128,8192]{1,0:T(8,128)} %bands.3) | copy-start | bytes 12582916
  2.8 79.1 %slice-start = ((s8[5242880]{0:T(1024)(128)(4,1)}), s8[4194304]{0:T(1024)(128)(4,1)S(1)}, s32[]{:S(2)}) async-start(s8[5242880]{0:T(1024)(128)(4,1)} %bitcast), calls=%async_computation | async-start | bytes 8388608
  2.9 77.9 %copy-start.1 = (f32[1,512,640]{2,1,0:T(8,128)S(1)}, f32[1,512,640]{2,1,0:T(8,128)}, u32[]{:S(2)}) copy-start(f32[1,512,640]{2,1,0:T(8,128)} %x_ref.2) | copy-start | bytes 3932164
  2.9 15.7 %collective-permute-start = (f32[128,768]{1,0:T(8,128)S(1)}, f32[128,768]{1,0:T(8,128)S(1)}, u32[]{:S(2)}, u32[]{:S(2)}) collective-permute-start(f32[128,768]{1,0:T(8,128)S(1)} %get-tuple-element.50), channel_id=1, source_target_pairs={{0,1},{1,0},{2,3},{3,2},{4,5},{5,4},{6,7},{7,6},{8,9},{9,8},{10,11... | collective-permute-start | bytes 1179656 | tf_op jit(solution)/shard_map/ppermute | solution.py:448
  3.1 19.3 %collective-permute-start.1 = (f32[128,768]{1,0:T(8,128)S(1)}, f32[128,768]{1,0:T(8,128)S(1)}, u32[]{:S(2)}, u32[]{:S(2)}) collective-permute-start(f32[128,768]{1,0:T(8,128)S(1)} %get-tuple-element.51), channel_id=1, source_target_pairs={{0,2},{1,3},{2,0},{3,1},{4,6},{5,7},{6,4},{7,5},{8,10},{9,11},{10,... | collective-permute-start | bytes 1179656 | tf_op jit(solution)/shard_map/ppermute | solution.py:448
  5.5 76.5 %slice-start.1 = ((s8[5242880]{0:T(1024)(128)(4,1)}), s8[1048576]{0:T(1024)(128)(4,1)S(1)}, s32[]{:S(2)}) async-start(s8[5242880]{0:T(1024)(128)(4,1)} %bitcast), calls=%async_computation.1 | async-start | bytes 2097152
  5.5 76.5 %copy-start.2 = (s32[4]{0:T(128)S(1)}, s32[4]{0:T(128)}, u32[]{:S(2)}) copy-start(s32[4]{0:T(128)} %start.2) | copy-start | bytes 52
  5.5 33.8 %collective-permute-start.2 = (f32[128,768]{1,0:T(8,128)S(1)}, f32[128,768]{1,0:T(8,128)S(1)}, u32[]{:S(2)}, u32[]{:S(2)}) collective-permute-start(f32[128,768]{1,0:T(8,128)S(1)} %get-tuple-element.52), channel_id=1, source_target_pairs={{0,3},{1,2},{2,1},{3,0},{4,7},{5,6},{6,5},{7,4},{8,11},{9,10},{10,... | collective-permute-start | bytes 1179656 | tf_op jit(solution)/shard_map/ppermute | solution.py:448
  5.9 56.6 %collective-permute-start.11 = (f32[128,768]{1,0:T(8,128)S(1)}, f32[128,768]{1,0:T(8,128)S(1)}, u32[]{:S(2)}, u32[]{:S(2)}) collective-permute-start(f32[128,768]{1,0:T(8,128)S(1)} %get-tuple-element.66), channel_id=1, source_target_pairs={{0,1},{1,0},{2,3},{3,2},{4,5},{5,4},{6,7},{7,6},{8,9},{9,8},{10,11... | collective-permute-start | bytes 1179656 | tf_op jit(solution)/shard_map/ppermute | solution.py:448
  7.1 56.7 %collective-permute-start.12 = (f32[128,768]{1,0:T(8,128)S(1)}, f32[128,768]{1,0:T(8,128)S(1)}, u32[]{:S(2)}, u32[]{:S(2)}) collective-permute-start(f32[128,768]{1,0:T(8,128)S(1)} %get-tuple-element.67), channel_id=1, source_target_pairs={{0,2},{1,3},{2,0},{3,1},{4,6},{5,7},{6,4},{7,5},{8,10},{9,11},{10,... | collective-permute-start | bytes 1179656 | tf_op jit(solution)/shard_map/ppermute | solution.py:448
  18.6 54.4 %collective-permute-start.13 = (f32[128,768]{1,0:T(8,128)S(1)}, f32[128,768]{1,0:T(8,128)S(1)}, u32[]{:S(2)}, u32[]{:S(2)}) collective-permute-start(f32[128,768]{1,0:T(8,128)S(1)} %get-tuple-element.68), channel_id=1, source_target_pairs={{0,3},{1,2},{2,1},{3,0},{4,7},{5,6},{6,5},{7,4},{8,11},{9,10},{10,... | collective-permute-start | bytes 1179656 | tf_op jit(solution)/shard_map/ppermute | solution.py:448
  39.4 38.6 %collective-permute-start.3 = (f32[128,768]{1,0:T(8,128)S(1)}, f32[128,768]{1,0:T(8,128)S(1)}, u32[]{:S(2)}, u32[]{:S(2)}) collective-permute-start(f32[128,768]{1,0:T(8,128)S(1)} %get-tuple-element.53), channel_id=1, source_target_pairs={{0,4},{8,12},{16,20},{24,28},{4,0},{12,8},{20,16},{28,24},{1,5},{9... | collective-permute-start | bytes 1179656 | tf_op jit(solution)/shard_map/ppermute | solution.py:424
  59.4 19.8 %collective-permute-start.4 = (f32[128,768]{1,0:T(8,128)S(1)}, f32[128,768]{1,0:T(8,128)S(1)}, u32[]{:S(2)}, u32[]{:S(2)}) collective-permute-start(f32[128,768]{1,0:T(8,128)S(1)} %get-tuple-element.54), channel_id=1, source_target_pairs={{4,8},{12,16},{20,24},{8,4},{16,12},{24,20},{5,9},{13,17},{21,25},... | collective-permute-start | bytes 1179656 | tf_op jit(solution)/shard_map/ppermute | solution.py:424
  62.5 36.2 %collective-permute-start.8 = (f32[128,768]{1,0:T(8,128)S(1)}, f32[128,768]{1,0:T(8,128)S(1)}, u32[]{:S(2)}, u32[]{:S(2)}) collective-permute-start(f32[128,768]{1,0:T(8,128)S(1)} %get-tuple-element.61), channel_id=1, source_target_pairs={{0,1},{3,2},{4,5},{7,6},{8,9},{11,10},{12,13},{15,14},{16,17},{19,... | collective-permute-start | bytes 1179656 | tf_op jit(solution)/shard_map/ppermute | solution.py:448
  73.1 19.4 %collective-permute-start.14 = (f32[128,768]{1,0:T(8,128)S(1)}, f32[128,768]{1,0:T(8,128)S(1)}, u32[]{:S(2)}, u32[]{:S(2)}) collective-permute-start(f32[128,768]{1,0:T(8,128)S(1)} %get-tuple-element.69), channel_id=1, source_target_pairs={{0,4},{8,12},{16,20},{24,28},{4,0},{12,8},{20,16},{28,24},{1,5},{9... | collective-permute-start | bytes 1179656 | tf_op jit(solution)/shard_map/ppermute | solution.py:424
  74.9 17.6 %collective-permute-start.15 = (f32[128,768]{1,0:T(8,128)S(1)}, f32[128,768]{1,0:T(8,128)S(1)}, u32[]{:S(2)}, u32[]{:S(2)}) collective-permute-start(f32[128,768]{1,0:T(8,128)S(1)} %get-tuple-element.70), channel_id=1, source_target_pairs={{4,8},{12,16},{20,24},{8,4},{16,12},{24,20},{5,9},{13,17},{21,25},... | collective-permute-start | bytes 1179656 | tf_op jit(solution)/shard_map/ppermute | solution.py:424
  77.9 20.8 %collective-permute-start.9 = (f32[128,768]{1,0:T(8,128)S(1)}, f32[128,768]{1,0:T(8,128)S(1)}, u32[]{:S(2)}, u32[]{:S(2)}) collective-permute-start(f32[128,768]{1,0:T(8,128)S(1)} %get-tuple-element.62), channel_id=1, source_target_pairs={{0,2},{3,1},{4,6},{7,5},{8,10},{11,9},{12,14},{15,13},{16,18},{19,... | collective-permute-start | bytes 1179656 | tf_op jit(solution)/shard_map/ppermute | solution.py:448
  79.3 19.5 %collective-permute-start.10 = (f32[128,768]{1,0:T(8,128)S(1)}, f32[128,768]{1,0:T(8,128)S(1)}, u32[]{:S(2)}, u32[]{:S(2)}) collective-permute-start(f32[128,768]{1,0:T(8,128)S(1)} %get-tuple-element.63), channel_id=1, source_target_pairs={{0,3},{3,0},{4,7},{7,4},{8,11},{11,8},{12,15},{15,12},{16,19},{19,... | collective-permute-start | bytes 1179656 | tf_op jit(solution)/shard_map/ppermute | solution.py:448
  98.8 16.0 %collective-permute-start.16 = (f32[144,768]{1,0:T(8,128)S(1)}, f32[144,768]{1,0:T(8,128)S(1)}, u32[]{:S(2)}, u32[]{:S(2)}) collective-permute-start(f32[144,768]{1,0:T(8,128)S(1)} %get-tuple-element.73), channel_id=1, source_target_pairs={{0,4},{8,12},{16,20},{24,28},{4,0},{12,8},{20,16},{28,24},{1,5},{9... | collective-permute-start | bytes 1327112 | tf_op jit(solution)/shard_map/ppermute | solution.py:424
  98.9 16.0 %collective-permute-start.17 = (f32[144,768]{1,0:T(8,128)S(1)}, f32[144,768]{1,0:T(8,128)S(1)}, u32[]{:S(2)}, u32[]{:S(2)}) collective-permute-start(f32[144,768]{1,0:T(8,128)S(1)} %get-tuple-element.74), channel_id=1, source_target_pairs={{4,8},{12,16},{20,24},{8,4},{16,12},{24,20},{5,9},{13,17},{21,25},... | collective-permute-start | bytes 1327112 | tf_op jit(solution)/shard_map/ppermute | solution.py:424
  102.4 24.4 %collective-permute-start.5 = (f32[128,768]{1,0:T(8,128)S(1)}, f32[128,768]{1,0:T(8,128)S(1)}, u32[]{:S(2)}, u32[]{:S(2)}) collective-permute-start(f32[128,768]{1,0:T(8,128)S(1)} %get-tuple-element.61), channel_id=1, source_target_pairs={{1,0},{2,3},{5,4},{6,7},{9,8},{10,11},{13,12},{14,15},{17,16},{18,... | collective-permute-start | bytes 1179656 | tf_op jit(solution)/shard_map/ppermute | solution.py:448
  110.3 16.5 %collective-permute-start.6 = (f32[128,768]{1,0:T(8,128)S(1)}, f32[128,768]{1,0:T(8,128)S(1)}, u32[]{:S(2)}, u32[]{:S(2)}) collective-permute-start(f32[128,768]{1,0:T(8,128)S(1)} %get-tuple-element.62), channel_id=1, source_target_pairs={{1,3},{2,0},{5,7},{6,4},{9,11},{10,8},{13,15},{14,12},{17,19},{18,... | collective-permute-start | bytes 1179656 | tf_op jit(solution)/shard_map/ppermute | solution.py:448
  112.6 17.3 %collective-permute-start.7 = (f32[128,768]{1,0:T(8,128)S(1)}, f32[128,768]{1,0:T(8,128)S(1)}, u32[]{:S(2)}, u32[]{:S(2)}) collective-permute-start(f32[128,768]{1,0:T(8,128)S(1)} %get-tuple-element.63), channel_id=1, source_target_pairs={{1,2},{2,1},{5,6},{6,5},{9,10},{10,9},{13,14},{14,13},{17,18},{18,... | collective-permute-start | bytes 1179656 | tf_op jit(solution)/shard_map/ppermute | solution.py:448
  114.8 15.1 %collective-permute-start.18 = (f32[8,512]{1,0:T(8,128)S(1)}, f32[8,512]{1,0:T(8,128)S(1)}, u32[]{:S(2)}, u32[]{:S(2)}) collective-permute-start(f32[8,512]{1,0:T(8,128)S(1)} %get-tuple-element.80), channel_id=1, source_target_pairs={{0,1},{2,3},{1,0},{3,2},{4,5},{6,7},{5,4},{7,6},{8,9},{10,11},{9,8... | collective-permute-start | bytes 49160 | tf_op jit(solution)/shard_map/ppermute | solution.py:424
  114.9 15.2 %collective-permute-start.19 = (f32[8,512]{1,0:T(8,128)S(1)}, f32[8,512]{1,0:T(8,128)S(1)}, u32[]{:S(2)}, u32[]{:S(2)}) collective-permute-start(f32[8,512]{1,0:T(8,128)S(1)} %get-tuple-element.80), channel_id=1, source_target_pairs={{1,2},{2,1},{5,6},{6,5},{9,10},{10,9},{13,14},{14,13},{17,18},{18,... | collective-permute-start | bytes 49160 | tf_op jit(solution)/shard_map/ppermute | solution.py:424
  132.6 17.3 %collective-permute-start.20 = (f32[16,1280]{1,0:T(8,128)S(1)}, f32[16,1280]{1,0:T(8,128)S(1)}, u32[]{:S(2)}, u32[]{:S(2)}) collective-permute-start(f32[16,1280]{1,0:T(8,128)S(1)} %get-tuple-element.90), channel_id=1, source_target_pairs={{0,4},{8,12},{16,20},{24,28},{4,0},{12,8},{20,16},{28,24},{1,5},{9... | collective-permute-start | bytes 245768 | tf_op jit(solution)/shard_map/ppermute | solution.py:424
  132.7 17.3 %collective-permute-start.21 = (f32[16,1280]{1,0:T(8,128)S(1)}, f32[16,1280]{1,0:T(8,128)S(1)}, u32[]{:S(2)}, u32[]{:S(2)}) collective-permute-start(f32[16,1280]{1,0:T(8,128)S(1)} %get-tuple-element.90), channel_id=1, source_target_pairs={{4,8},{12,16},{20,24},{8,4},{16,12},{24,20},{5,9},{13,17},{21,25},... | collective-permute-start | bytes 245768 | tf_op jit(solution)/shard_map/ppermute | solution.py:424
